TPU v7x, 32 devices: a whole 2x2x4 slice. The times are simulated.
32 devices in a mesh: grp: 2 (over y), depth: 4 (over x, core), shot: 4 (over z).
Axes of the slice: x: 2, y: 2, z: 4, core: 2. Of those that a mesh axis runs over, the one named last changes fastest.
Arguments:
- forward: bfloat16 [4, 8, 32, 32, 128], P(None, ('grp', 'shot'), 'depth'), parts along dimension 1, may hold values from -6 to 6
- adjoint_last: float32 [8, 32, 32, 128], P(('grp', 'shot'), 'depth'), parts along dimension 0, may hold values from -6 to 6
- adjoint_late: float32 [8, 32, 32, 128], P(('grp', 'shot'), 'depth'), parts along dimension 0, may hold values from -6 to 6
- residuals: float32 [8, 4, 256], P(('grp', 'shot')), parts along dimension 0, may hold values from -6 to 6
- source_cells: int32 [8, 3], P('grp'), parts along dimension 0, may hold values from 0 to 127, as said below
- receiver_cells: int32 [8, 256, 3], P('grp'), parts along dimension 0, may hold values from 0 to 127, as said below
- assignment: int32 [8], P('grp'), parts along dimension 0, may hold values from 0 to 3, each once
- model: float32 [6, 32, 16, 64], P(None, ('grp', 'depth'), 'shot'), parts along dimension 1, may hold values from -0.4 to 2, as said below
Outputs:
- adjoint_first: float32 [8, 32, 32, 128], P(('grp', 'shot'), 'depth'), parts along dimension 0
- gradients: float32 [6, 32, 16, 64], P(None, ('grp', 'depth'), 'shot'), parts along dimension 1
There are 2 independent parts, one for each index of `grp`. A program takes and returns all parts, laid end to end along the dimension named above; each array names one. Nothing has to cross between parts.
Inputs may be any that keep to these rules, and one draw needn't show every extreme that they name: `source_cells`: each row holds the depth, second and third cell index of a source inside the grid of 32 x 32 x 128 cells. `receiver_cells`: each entry holds the depth, second and third cell index of a receiver inside the grid; receivers may share a cell. `assignment`: each survey row is used by exactly one shot. `model`: channel 0 (depth with depth) lies in 1 to 2; channels 1 and 2 (second with second, third with third) lie in 0.25 to 1; channels 3 to 5 (depth with second, depth with third, second with third) lie in -0.4 to 0.4.
All inputs are finite; a program needn't handle non-finite values.
Results may differ from a plain program's by a relative error of at most 0.0003.
Values sent between devices are 32-bit elements; how exact they have to be, the bound alone decides.
No kernel may reach another device: no remote copies, remote signals or barrier semaphores. Data moves between devices by JAX's collectives and lax.ppermute only.
A program may use at most 128 MiB of HBM per device.

v0:
```python
import jax
import jax.numpy as jnp
from jax import lax
from jax.sharding import PartitionSpec as P

MUTE = 3


TIME_SQUARED = 0.2


def extended_2(array, sides, width):
    for axis, dim in sides:
        devices, length = (lax.axis_size(axis), array.shape[dim])
        up = [(i, (i + 1) % devices) for i in range(devices - 1)]
        down = [(j, i) for i, j in up]
        last = lax.slice_in_dim(array, length - width, length, axis=dim)
        leading = lax.slice_in_dim(array, 0, width, axis=dim)
        before = lax.ppermute(last, axis, up)
        after = lax.ppermute(leading, axis, down)
        array = jnp.concatenate([before, array, after], axis=dim)
    return array


def passed_along(array, axis, by):
    devices = lax.axis_size(axis)
    pairs = [(i, i + by) for i in range(devices) if 0 <= i + by < devices]
    return lax.ppermute(array, axis, pairs)


def refine(coarse, dimension):
    coarse_count = coarse.shape[dimension]
    later_rows = lax.slice_in_dim(coarse, 1, coarse_count, axis=dimension)
    edge_row = lax.slice_in_dim(coarse, coarse_count - 1, coarse_count, axis=dimension)
    middle = (coarse + jnp.concatenate([later_rows, edge_row], axis=dimension)) * 0.5
    merged = jnp.stack([coarse, middle], axis=dimension + 1)
    new_shape = coarse.shape[:dimension] + (2 * coarse_count,) + coarse.shape[dimension + 1 :]
    return merged.reshape(new_shape)


def coarsen(fine_cells, dimension):
    half_count = fine_cells.shape[dimension] // 2
    paired = fine_cells.reshape(
        fine_cells.shape[:dimension] + (half_count, 2) + fine_cells.shape[dimension + 1 :]
    )
    even_cells = lax.index_in_dim(paired, 0, dimension + 1, keepdims=False)
    odd_cells = lax.index_in_dim(paired, 1, dimension + 1, keepdims=False)
    first_odd = lax.slice_in_dim(odd_cells, 0, 1, axis=dimension)
    earlier = jnp.concatenate(
        [jnp.zeros_like(first_odd), lax.slice_in_dim(odd_cells, 0, half_count - 1, axis=dimension)],
        axis=dimension,
    )
    tail_part = jnp.concatenate(
        [
            jnp.zeros_like(lax.slice_in_dim(odd_cells, 1, half_count, axis=dimension)),
            lax.slice_in_dim(odd_cells, half_count - 1, half_count, axis=dimension),
        ],
        axis=dimension,
    )
    return even_cells + 0.5 * odd_cells + 0.5 * earlier + 0.5 * tail_part


def coarsen_depth(fine_cells, rim_layer, last_scale):
    half_count = fine_cells.shape[1] // 2
    paired = fine_cells.reshape((fine_cells.shape[0], half_count, 2) + fine_cells.shape[2:])
    even_cells = paired[:, :, 0]
    odd_cells = paired[:, :, 1]
    earlier = jnp.concatenate([rim_layer, odd_cells[:, : half_count - 1]], axis=1)
    tail_part = jnp.concatenate(
        [jnp.zeros_like(odd_cells[:, 1:]), odd_cells[:, half_count - 1 :]], axis=1
    )
    return even_cells + 0.5 * odd_cells + 0.5 * earlier + last_scale * tail_part


def window(padded, offsets):
    depth_step, row_step, column_step = offsets
    inner_depth = padded.shape[-3] - 2
    inner_rows = padded.shape[-2] - 2
    inner_columns = padded.shape[-1] - 2
    return padded[
        ...,
        1 + depth_step : 1 + depth_step + inner_depth,
        1 + row_step : 1 + row_step + inner_rows,
        1 + column_step : 1 + column_step + inner_columns,
    ]


def derivatives(padded):
    centre = window(padded, (0, 0, 0))

    def second(offsets, opposite):
        return window(padded, offsets) - 2.0 * centre + window(padded, opposite)

    def cross(upper_one, upper_two, lower_one, lower_two):
        return (
            window(padded, upper_one)
            - window(padded, upper_two)
            - window(padded, lower_one)
            + window(padded, lower_two)
        ) * 0.25

    return jnp.stack(
        [
            second((1, 0, 0), (-1, 0, 0)),
            second((0, 1, 0), (0, -1, 0)),
            second((0, 0, 1), (0, 0, -1)),
            cross((1, 1, 0), (1, -1, 0), (-1, 1, 0), (-1, -1, 0)),
            cross((1, 0, 1), (1, 0, -1), (-1, 0, 1), (-1, 0, -1)),
            cross((0, 1, 1), (0, 1, -1), (0, -1, 1), (0, -1, -1)),
        ],
        axis=0,
    )


def side_pad(wave_field):
    return jnp.pad(wave_field, ((0, 0), (0, 0), (1, 1), (1, 1)))


def inject(wave_field, receivers, values, depth_first):
    shots_here, depth_len, row_len, column_len = wave_field.shape
    local_depth = receivers[..., 0] - depth_first
    inside = (local_depth >= 0) & (local_depth < depth_len)
    shot_rows = jnp.arange(shots_here, dtype=jnp.int32)[:, None]
    flat_index = (
        (shot_rows * depth_len + local_depth) * row_len + receivers[..., 1]
    ) * column_len + receivers[..., 2]
    flat_index = jnp.where(inside, flat_index, wave_field.size)
    added = wave_field.reshape(-1).at[flat_index.reshape(-1)].add(values.reshape(-1), mode="drop")
    return added.reshape(wave_field.shape)


def on_device(
    forward, adjoint_last, adjoint_late, residuals, source_cells, receiver_cells, assignment, model
):
    steps_total = forward.shape[0]
    shots_here, depth_len, row_len, column_len = adjoint_last.shape
    depth_index = lax.axis_index("depth")
    depth_count = lax.axis_size("depth")
    last_depth = depth_index == depth_count - 1
    last_scale = jnp.where(last_depth, 0.5, 0.0).astype(jnp.float32)
    depth_first = depth_index * depth_len
    current, previous = (adjoint_last, adjoint_late)
    reach = steps_total // 2 + 1
    coarse_total = depth_count * depth_len // 2
    fine_total = depth_count * depth_len
    coarse_first = depth_index * (depth_len // 2) - reach
    fine_offset = 2 * reach - steps_total
    fine_count = depth_len + 2 * steps_total
    extended = extended_2(model, (("depth", 1),), reach)
    piece = lax.all_gather(extended, "shot", axis=2, tiled=True)
    count = piece.shape[1]
    global_rows = coarse_first + jnp.arange(count, dtype=jnp.int32)
    later_rows = jnp.concatenate([piece[:, 1:], jnp.zeros_like(piece[:, :1])], axis=1)
    following = jnp.where((global_rows == coarse_total - 1)[None, :, None, None], piece, later_rows)
    middle = (piece + following) * 0.5
    deeper = jnp.stack([piece, middle], axis=2).reshape(
        (piece.shape[0], 2 * count) + piece.shape[2:]
    )
    sliced = deeper[:, fine_offset : fine_offset + fine_count]
    fine_rows = 2 * coarse_first + fine_offset + jnp.arange(fine_count, dtype=jnp.int32)
    inside = (fine_rows >= 0) & (fine_rows < fine_total)
    sliced = jnp.where(inside[None, :, None, None], sliced, jnp.zeros_like(sliced))
    gathered = refine(sliced, 3)
    used_coefficients = refine(gathered, 2)
    both_fields = extended_2(jnp.stack([current, previous]), (("depth", 2),), steps_total)
    current, previous = (both_fields[0], both_fields[1])
    survey_count = assignment.shape[0]
    survey_ids = jnp.arange(survey_count, dtype=jnp.int32)
    shot_ids = lax.axis_index("shot") * shots_here + jnp.arange(shots_here, dtype=jnp.int32)
    geometry = jnp.sum(
        jnp.where(survey_ids[None, :] == shot_ids[:, None], assignment[None, :], 0), axis=1
    )
    chosen = survey_ids[None, :] == geometry[:, None]
    sources = jnp.sum(jnp.where(chosen[:, :, None], source_cells[None], 0), axis=1)
    receivers = jnp.sum(jnp.where(chosen[:, :, None, None], receiver_cells[None], 0), axis=1)
    depth_cells = depth_first + jnp.arange(depth_len, dtype=jnp.int32)
    row_cells = jnp.arange(row_len, dtype=jnp.int32)
    column_cells = jnp.arange(column_len, dtype=jnp.int32)
    muted = (
        (jnp.abs(depth_cells[None, :] - sources[:, 0:1]) <= MUTE)[:, :, None, None]
        & (jnp.abs(row_cells[None, :] - sources[:, 1:2]) <= MUTE)[:, None, :, None]
        & (jnp.abs(column_cells[None, :] - sources[:, 2:3]) <= MUTE)[:, None, None, :]
    )
    totals = jnp.zeros((6, shots_here, depth_len, row_len, column_len), jnp.float32)
    for step_index in range(steps_total):
        slopes = derivatives(side_pad(jnp.pad(current, ((0, 0), (1, 1), (0, 0), (0, 0)))))
        owned_slopes = slopes[:, :, steps_total : steps_total + depth_len]
        term = forward[step_index].astype(jnp.float32)[None] * owned_slopes
        totals = totals + term
        updated = (
            2.0 * current
            - previous
            + TIME_SQUARED * jnp.sum(used_coefficients[:, None] * slopes, axis=0)
        )
        updated = inject(updated, receivers, residuals[:, step_index], depth_first - steps_total)
        previous, current = (current, updated)
    kept = jnp.sum(jnp.where(muted[None], jnp.zeros_like(totals), totals), axis=1)
    coarse_rows = coarsen(coarsen(kept, 3), 2)
    rim_layer = passed_along(coarse_rows[:, depth_len - 1 :], "depth", 1)
    gradients = lax.psum_scatter(
        coarsen_depth(coarse_rows, rim_layer, last_scale), "shot", scatter_dimension=2, tiled=True
    )
    adjoint_first = current[:, steps_total : steps_total + depth_len]
    return (adjoint_first, gradients / steps_total)


def solution(mesh):
    placed = (
        P(None, ("grp", "shot"), "depth", None, None),
        P(("grp", "shot"), "depth", None, None),
        P(("grp", "shot"), "depth", None, None),
        P(("grp", "shot"), None, None),
        P("grp", None),
        P("grp", None, None),
        P("grp"),
        P(None, ("grp", "depth"), "shot", None),
    )
    return jax.shard_map(
        on_device,
        mesh=mesh,
        in_specs=placed,
        out_specs=(
            P(("grp", "shot"), "depth", None, None),
            P(None, ("grp", "depth"), "shot", None),
        ),
        check_vma=False,
    )
```

profile of v0, /device:TPU:0, one launch (start us, length us, event | category | flops | bytes accessed | tf_op | source)
XLA Modules:
  0.0 177.3 jit_solution(18199098292120019333)
XLA Ops:
  7.2 0.8 copy.373
  8.1 2.4 %collective-permute-start.2 = (f32[6,3,4,64]{3,0,1,2:T(8,128)S(1)}, f32[6,3,4,64]{3,0,1,2:T(8,128)S(1)}, u32[]{:S(2)}, u32[]{:S(2)}) collective-permute-start(f32[6,3,4,64]{3,0,1,2:T(8,128)S(1)} %get-tuple-element.59), channel_id=1, source_target_pairs={{0,4},{4,8},{8,12},{1,5},{5,9},{9,13},{2,6},{6,10},{10,14},{3,7},{... | collective-permute-start | bytes 55304 | tf_op jit(solution)/shard_map/ppermute | solution.py:19
  10.5 1.3 collective-permute-start.3
  11.8 1.0 fusion.82
  12.7 5.1 %collective-permute-start = (f32[2,1,4,32,128]{4,3,2,1,0:T(8,128)S(1)}, f32[2,1,4,32,128]{4,3,2,1,0:T(8,128)S(1)}, u32[]{:S(2)}, u32[]{:S(2)}) collective-permute-start(f32[2,1,4,32,128]{4,3,2,1,0:T(8,128)S(1)} %get-tuple-element.57), channel_id=1, source_target_pairs={{0,4},{4,8},{8,12},{1,5},{5,9},{9,13},{2,6},{6,10},{10,14},{3,7},{... | collective-permute-start | bytes 393224 | tf_op jit(solution)/shard_map/ppermute | solution.py:19
  17.9 1.3 collective-permute-start.1
  19.2 1.3 fusion.84
  20.5 0.6 iota_compare_fusion
  21.1 0.8 fusion.107
  22.0 0.8 select_reduce_fusion
  22.8 0.8 select_reduce_fusion.1
  23.5 0.6 fusion.108
  24.1 0.7 abs_compare_fusion.2
  24.8 0.6 abs_compare_fusion.1
  25.4 0.7 abs_compare_fusion
  26.1 1.7 bitcast_convert_fusion.3
  27.9 0.7 broadcast_and_fusion
  28.6 0.6 dynamic-slice
  29.9 17.3 %all_gather.3 = f32[6,10,16,64]{3,0,1,2:T(8,128)S(1)} all-gather(f32[6,10,4,64]{3,0,1,2:T(8,128)S(1)} %pad_maximum_fusion.4), channel_id=1, replica_groups=mesh['grp'=2,'depth'=4,'shot'=4] {'shot'}, dimensions={2}, use_global_device_ids=true | all-gather | bytes 307200 | tf_op jit(solution)/shard_map/all_gather | solution.py:150
  49.0 6.1 %copy.380 = f32[6,16,16,64,2]{2,1,4,3,0:T(8,128)} copy(f32[6,16,16,64,2]{3,2,1,0,4:T(8,128)S(1)} %pad_maximum_fusion) | data formatting | bytes 1572864 | tf_op jit(solution)/shard_map/stack | solution.py:36
  55.2 7.2 %slice.500 = f32[6,16,1,128]{2,1,3,0:T(8,128)} slice(f32[6,16,16,128]{2,1,3,0:T(8,128)} %bitcast.178), slice={[0:6], [0:16], [15:16], [0:128]} | slice | bytes 98304 | tf_op jit(solution)/shard_map/slice | solution.py:34
  62.4 4.3 %slice_bitcast_fusion = f32[6,16,15,1,128]{2,1,4,0,3:T(8,128)} fusion(f32[6,16,16,128]{2,1,3,0:T(8,128)S(1)} %bitcast.181), kind=kLoop, calls=%fused_computation.4 | loop fusion | bytes 1474560 | tf_op jit(solution)/shard_map/concatenate | solution.py:35
  66.7 4.7 %copy.382 = f32[6,16,1,128]{3,1,0,2:T(8,128)S(1)} copy(f32[6,16,1,128]{2,1,3,0:T(8,128)} %slice.500) | data formatting | bytes 98304 | tf_op jit(solution)/shard_map/slice | solution.py:34
  71.4 4.2 %copy.383 = f32[6,16,1,1,128]{2,1,4,0,3:T(8,128)} copy(f32[6,16,1,1,128]{4,1,0,3,2:T(8,128)S(1)} %bitcast.240) | data formatting | bytes 98304 | tf_op jit(solution)/shard_map/concatenate | solution.py:35
  75.6 10.7 %fusion = f32[6,16,16,1,128]{2,1,4,0,3:T(8,128)} fusion(f32[6,16,16,1,128]{2,1,4,0,3:T(8,128)} %bitcast.179, f32[6,16,1,1,128]{2,1,4,0,3:T(8,128)} %copy.383, f32[6,16,15,1,128]{2,1,4,0,3:T(8,128)} %slice_bitcast_fusion), kind=kLoop, calls=%fused_computation.6 | loop fusion | flops 589824 | bytes 2359296 | tf_op jit(solution)/shard_map/mul | solution.py:35
  86.3 4.6 %copy.384 = f32[6,16,16,1,128]{4,2,3,1,0:T(8,128)S(1)} copy(f32[6,16,16,1,128]{2,1,4,0,3:T(8,128)} %bitcast.180) | data formatting | bytes 1572864 | tf_op jit(solution)/shard_map/stack;reshape | solution.py:36
  90.9 4.7 %copy.385 = f32[6,16,16,1,128]{4,2,3,1,0:T(8,128)S(1)} copy(f32[6,16,16,1,128]{2,1,4,0,3:T(8,128)} %fusion) | data formatting | bytes 1572864 | tf_op jit(solution)/shard_map/mul | solution.py:35
  97.0 1.0 copy-done.10
  98.5 2.3 %scatter_fusion = f32[65536]{0:T(1024)S(1)} fusion(f32[65536]{0:T(1024)S(1)} %subtract_add_fusion.3, s32[256]{0:T(256)S(1)} %bitcast.242, f32[256]{0:T(256)S(1)} %bitcast.251), kind=kCustom, calls=%fused_computation | custom fusion | flops 256 | bytes 4096 | tf_op jit(solution)/shard_map/scatter-add | solution.py:128
  102.1 1.0 copy-done.6
  103.7 2.1 %scatter_fusion.1 = f32[65536]{0:T(1024)S(1)} fusion(f32[65536]{0:T(1024)S(1)} %subtract_add_fusion.2, s32[256]{0:T(256)S(1)} %bitcast.243, f32[256]{0:T(256)S(1)} %bitcast.250), kind=kCustom, calls=%fused_computation.1 | custom fusion | flops 256 | bytes 4096 | tf_op jit(solution)/shard_map/scatter-add | solution.py:128
  107.1 1.0 copy-done.8
  108.6 2.1 %scatter_fusion.2 = f32[65536]{0:T(1024)S(1)} fusion(f32[65536]{0:T(1024)S(1)} %subtract_add_fusion.1, s32[256]{0:T(256)S(1)} %bitcast.244, f32[256]{0:T(256)S(1)} %bitcast.249), kind=kCustom, calls=%fused_computation.2 | custom fusion | flops 256 | bytes 4096 | tf_op jit(solution)/shard_map/scatter-add | solution.py:128
  110.8 0.8 bitcast_dynamic-update-slice_fusion.4
  111.6 0.9 bitcast_dynamic-update-slice_fusion.3
  112.6 1.0 bitcast_dynamic-update-slice_fusion.1
  113.6 1.0 bitcast_dynamic-update-slice_fusion
  115.2 2.2 %copy.446 = f32[6,1,8,32,128]{3,2,4,0,1:T(8,128)} copy(f32[6,1,8,32,128]{4,3,2,1,0:T(8,128)S(1)} %fusion.5) | data formatting | bytes 1572864 | tf_op jit(solution)/shard_map/jit(_where)/select_n | solution.py:197
  117.4 1.5 slice_bitcast_fusion.1
  119.0 1.8 copy-done.1
  120.8 1.4 fusion.3
  122.2 1.9 %copy.451 = f32[6,8,32,64]{3,1,2,0:T(8,128)S(1)} copy(f32[6,8,32,64]{2,1,3,0:T(8,128)} %fusion.3) | data formatting | bytes 786432 | tf_op jit(solution)/shard_map/add | solution.py:60
  124.4 3.0 %collective-permute-start.4 = (f32[6,1,16,64]{3,1,2,0:T(1,128)S(1)}, f32[6,1,16,64]{3,1,2,0:T(1,128)S(1)}, u32[]{:S(2)}, u32[]{:S(2)}) collective-permute-start(f32[6,1,16,64]{3,1,2,0:T(1,128)S(1)} %slice.519), channel_id=1, source_target_pairs={{0,4},{4,8},{8,12},{1,5},{5,9},{9,13},{2,6},{6,10},{10,14},{3,7},{... | collective-permute-start | bytes 73736 | tf_op jit(solution)/shard_map/ppermute | solution.py:28
  128.3 0.7 fusion.81
  129.1 2.1 %scatter_fusion.3 = f32[65536]{0:T(1024)S(1)} fusion(f32[65536]{0:T(1024)S(1)} %subtract_add_fusion, s32[256]{0:T(256)S(1)} %bitcast.245, f32[256]{0:T(256)S(1)} %bitcast.248), kind=kCustom, calls=%fused_computation.3 | custom fusion | flops 256 | bytes 4096 | tf_op jit(solution)/shard_map/scatter-add | solution.py:128
  131.2 0.7 slice.504
  131.9 37.1 %all-reduce.17.cloned.1.call-done = f32[6,4,16,64]{3,2,1,0:T(8,128)} async-done(((f32[6,4,16,64]{3,2,1,0:T(8,128)}), f32[6,4,16,64]{3,2,1,0:T(8,128)}) %all-reduce.17.cloned.1.call-update) | async-done | bytes 98320
  169.0 1.5 dynamic-slice_multiply_fusion
  (136 shorter events, 9.0 us)
Async XLA Ops:
  7.2 21.4 %copy-start.18 = (u32[32]{0:T(128)S(1)}, u32[32]{0:T(128)}, u32[]{:S(2)}) copy-start(u32[32]{0:T(128)} %constant.101) | copy-start | bytes 388
  7.2 161.8 %all-reduce.17.cloned.1.call-start = ((), (), s32[]{:S(2)}) async-start(), calls=%async_computation | async-start | bytes 393216
  8.1 21.8 %collective-permute-start.2 = (f32[6,3,4,64]{3,0,1,2:T(8,128)S(1)}, f32[6,3,4,64]{3,0,1,2:T(8,128)S(1)}, u32[]{:S(2)}, u32[]{:S(2)}) collective-permute-start(f32[6,3,4,64]{3,0,1,2:T(8,128)S(1)} %get-tuple-element.59), channel_id=1, source_target_pairs={{0,4},{4,8},{8,12},{1,5},{5,9},{9,13},{2,6},{6,10},{10,14},{3,7},{... | collective-permute-start | bytes 55304 | tf_op jit(solution)/shard_map/ppermute | solution.py:19
  10.5 19.4 %collective-permute-start.3 = (f32[6,3,4,64]{3,0,1,2:T(8,128)S(1)}, f32[6,3,4,64]{3,0,1,2:T(8,128)S(1)}, u32[]{:S(2)}, u32[]{:S(2)}) collective-permute-start(f32[6,3,4,64]{3,0,1,2:T(8,128)S(1)} %get-tuple-element.60), channel_id=1, source_target_pairs={{4,0},{8,4},{12,8},{5,1},{9,5},{13,9},{6,2},{10,6},{14,10},{7,3},{... | collective-permute-start | bytes 55304 | tf_op jit(solution)/shard_map/ppermute | solution.py:20
  12.7 82.8 %collective-permute-start = (f32[2,1,4,32,128]{4,3,2,1,0:T(8,128)S(1)}, f32[2,1,4,32,128]{4,3,2,1,0:T(8,128)S(1)}, u32[]{:S(2)}, u32[]{:S(2)}) collective-permute-start(f32[2,1,4,32,128]{4,3,2,1,0:T(8,128)S(1)} %get-tuple-element.57), channel_id=1, source_target_pairs={{0,4},{4,8},{8,12},{1,5},{5,9},{9,13},{2,6},{6,10},{10,14},{3,7},{... | collective-permute-start | bytes 393224 | tf_op jit(solution)/shard_map/ppermute | solution.py:19
  17.9 77.7 %collective-permute-start.1 = (f32[2,1,4,32,128]{4,3,2,1,0:T(8,128)S(1)}, f32[2,1,4,32,128]{4,3,2,1,0:T(8,128)S(1)}, u32[]{:S(2)}, u32[]{:S(2)}) collective-permute-start(f32[2,1,4,32,128]{4,3,2,1,0:T(8,128)S(1)} %get-tuple-element.58), channel_id=1, source_target_pairs={{4,0},{8,4},{12,8},{5,1},{9,5},{13,9},{6,2},{10,6},{14,10},{7,3},{... | collective-permute-start | bytes 393224 | tf_op jit(solution)/shard_map/ppermute | solution.py:20
  55.2 7.2 %copy-start = (f32[6,16,16,64,2]{2,1,4,3,0:T(8,128)S(1)}, f32[6,16,16,64,2]{2,1,4,3,0:T(8,128)}, u32[]{:S(2)}) copy-start(f32[6,16,16,64,2]{2,1,4,3,0:T(8,128)} %copy.380) | copy-start | bytes 2359300
  90.9 4.7 %copy-start.15 = (f32[1,8,32,128]{3,2,1,0:T(8,128)S(1)}, f32[1,8,32,128]{3,2,1,0:T(8,128)}, u32[]{:S(2)}) copy-start(f32[1,8,32,128]{3,2,1,0:T(8,128)} %param.9) | copy-start | bytes 393220
  90.9 4.7 %copy-start.16 = (f32[1,8,32,128]{3,2,1,0:T(8,128)S(1)}, f32[1,8,32,128]{3,2,1,0:T(8,128)}, u32[]{:S(2)}) copy-start(f32[1,8,32,128]{3,2,1,0:T(8,128)} %param.10) | copy-start | bytes 393220
  96.9 1.2 copy-start.10
  102.0 1.1 copy-start.6
  106.9 1.2 copy-start.8
  110.8 3.9 %copy-start.11 = (f32[6,1,16,32,128]{4,3,2,1,0:T(8,128)S(1)}, f32[6,1,16,32,128]{4,3,2,1,0:T(8,128)}, u32[]{:S(2)}) copy-start(f32[6,1,16,32,128]{4,3,2,1,0:T(8,128)} %copy-done.10) | copy-start | bytes 4718596
  110.8 3.9 %copy-start.17 = (pred[8,32,128]{2,1,0:T(8,128)(4,1)S(1)}, pred[8,32,128]{2,1,0:T(8,128)(4,1)}, u32[]{:S(2)}) copy-start(pred[8,32,128]{2,1,0:T(8,128)(4,1)} %broadcast_and_fusion) | copy-start | bytes 98308
  111.6 3.1 %copy-start.7 = (f32[6,1,16,32,128]{4,3,2,1,0:T(8,128)S(1)}, f32[6,1,16,32,128]{4,3,2,1,0:T(8,128)}, u32[]{:S(2)}) copy-start(f32[6,1,16,32,128]{4,3,2,1,0:T(8,128)} %copy-done.6) | copy-start | bytes 4718596
  111.6 3.1 %copy-start.9 = (f32[6,1,16,32,128]{4,3,2,1,0:T(8,128)S(1)}, f32[6,1,16,32,128]{4,3,2,1,0:T(8,128)}, u32[]{:S(2)}) copy-start(f32[6,1,16,32,128]{4,3,2,1,0:T(8,128)} %copy-done.8) | copy-start | bytes 4718596
  111.6 3.1 %copy-start.12 = (f32[8,32,128]{2,1,0:T(8,128)S(1)}, f32[8,32,128]{2,1,0:T(8,128)}, u32[]{:S(2)}) copy-start(f32[8,32,128]{2,1,0:T(8,128)} %get-tuple-element.54) | copy-start | bytes 393220
  111.6 3.1 %copy-start.13 = (f32[8,32,128]{2,1,0:T(8,128)S(1)}, f32[8,32,128]{2,1,0:T(8,128)}, u32[]{:S(2)}) copy-start(f32[8,32,128]{2,1,0:T(8,128)} %get-tuple-element.55) | copy-start | bytes 393220
  111.6 3.1 %copy-start.14 = (f32[8,32,128]{2,1,0:T(8,128)S(1)}, f32[8,32,128]{2,1,0:T(8,128)}, u32[]{:S(2)}) copy-start(f32[8,32,128]{2,1,0:T(8,128)} %get-tuple-element.56) | copy-start | bytes 393220
  118.9 1.9 %copy-start.1 = (f32[6,1,8,32,128]{3,2,4,0,1:T(8,128)S(1)}, f32[6,1,8,32,128]{3,2,4,0,1:T(8,128)}, u32[]{:S(2)}) copy-start(f32[6,1,8,32,128]{3,2,4,0,1:T(8,128)} %copy.446) | copy-start | bytes 2359300
  124.2 3.3 %copy-start.4 = (f32[1,16,32,128]{3,2,1,0:T(8,128)S(1)}, f32[1,16,32,128]{3,2,1,0:T(8,128)}, u32[]{:S(2)}) copy-start(f32[1,16,32,128]{3,2,1,0:T(8,128)} %get-tuple-element.47) | copy-start | bytes 786436
  124.2 3.4 %copy-start.5 = (f32[1,16,32,128]{3,2,1,0:T(8,128)S(1)}, f32[1,16,32,128]{3,2,1,0:T(8,128)}, u32[]{:S(2)}) copy-start(f32[1,16,32,128]{3,2,1,0:T(8,128)} %get-tuple-element.45) | copy-start | bytes 786436
  124.3 3.3 %copy-start.2 = (f32[1,16,32,128]{3,2,1,0:T(8,128)S(1)}, f32[1,16,32,128]{3,2,1,0:T(8,128)}, u32[]{:S(2)}) copy-start(f32[1,16,32,128]{3,2,1,0:T(8,128)} %get-tuple-element.41) | copy-start | bytes 786436
  124.3 3.4 %copy-start.3 = (f32[1,16,32,128]{3,2,1,0:T(8,128)S(1)}, f32[1,16,32,128]{3,2,1,0:T(8,128)}, u32[]{:S(2)}) copy-start(f32[1,16,32,128]{3,2,1,0:T(8,128)} %get-tuple-element.39) | copy-start | bytes 786436
  124.4 3.9 %collective-permute-start.4 = (f32[6,1,16,64]{3,1,2,0:T(1,128)S(1)}, f32[6,1,16,64]{3,1,2,0:T(1,128)S(1)}, u32[]{:S(2)}, u32[]{:S(2)}) collective-permute-start(f32[6,1,16,64]{3,1,2,0:T(1,128)S(1)} %slice.519), channel_id=1, source_target_pairs={{0,4},{4,8},{8,12},{1,5},{5,9},{9,13},{2,6},{6,10},{10,14},{3,7},{... | collective-permute-start | bytes 73736 | tf_op jit(solution)/shard_map/ppermute | solution.py:28
Sparse Core Ops, SparseCore 0:
  129.2 39.6 all-reduce.16
where the time goes:
time: 178 us; the launch traced here: 177 us
  local copies, waits for them, and re-layouts  52.1 us (29%)
  other arithmetic  41.9 us (24%)
  waiting for transfers between devices  37.2 us (21%)
  blocking collectives  17.3 us (10%)
  between operations  15.6 us (9%)
  starting transfers between devices  13.2 us (7%)
    unnamed x2, waiting for transfers between devices  37.1 us
    all_gather x1, blocking collectives, on_device(): piece = lax.all_gather(extended, 'shot', axis=2, tiled=True)  17.3 us
    slice x3, local copies, waits for them, and re-layouts, refine(): lax.slice_in_dim(coarse, coarse_count - 1, coarse_count, axis=dimension)  12.2 us
    another operation x2, local copies, waits for them, and re-layouts, refine(): merged = jnp.stack([coarse, middle], axis=dimension + 1)  10.8 us
    mul x1, other arithmetic, refine(): (coarse + jnp.concatenate([later_rows, edge_row], axis=dimension)) * 0.5  10.7 us
    scatter-add x4, other arithmetic, inject(): wave_field.reshape(-1).at[flat_index.reshape(-1)]  8.5 us
    concatenate x2, local copies, waits for them, and re-layouts, refine(): jnp.concatenate([later_rows, edge_row], axis=dimension)  8.48 us
    ppermute x2, starting transfers between devices, extended_2(): before = lax.ppermute(last, axis, up)  7.53 us
  transfers between devices with their start and end apart: 6, of which 2 were waited for; matrix products, arithmetic and copies ran while one was open for 35% of the time, Pallas kernels for 0%

commit v1 on v0

v1 whole, which is shorter than its diff:
```python
import functools

import jax
import jax.numpy as jnp
from jax import lax
from jax.experimental import pallas as pl
from jax.experimental.pallas import tpu as pltpu
from jax.sharding import PartitionSpec as P

MUTE = 3
TIME_SQUARED = 0.2
PAD = 8
VMEM = pl.BlockSpec(memory_space=pltpu.VMEM)
SMEM = pl.BlockSpec(memory_space=pltpu.SMEM)


def refine_matrix(coarse):
    row = lax.broadcasted_iota(jnp.int32, (coarse, 2 * coarse), 0)
    column = lax.broadcasted_iota(jnp.int32, (coarse, 2 * coarse), 1)
    here = column // 2
    after = jnp.minimum(here + 1, coarse - 1)
    odd = (column % 2) == 1
    at_here = jnp.where(row == here, 1.0, 0.0)
    at_after = jnp.where(row == after, 1.0, 0.0)
    return jnp.where(odd, 0.5 * (at_here + at_after), at_here).astype(jnp.float32)


def exact_dot(left, right, contract):
    return lax.dot_general(
        left,
        right,
        (contract, ((), ())),
        precision=lax.Precision.HIGHEST,
        preferred_element_type=jnp.float32,
    )


def even_depth():
    return lax.axis_index("depth") % 2 == 0


def pack_model(model_ref, own_ref, first_ref, second_ref, staged, *, reach):
    channels, depth_len, rows, _ = model_ref.shape
    for z in range(depth_len):
        for k in range(channels):
            at = (z * channels + k) * rows
            staged[at : at + rows, :] = model_ref[k, z]
    own_ref[...] = exact_dot(staged[...], refine_matrix(model_ref.shape[3]), ((1,), (0,)))
    part = reach * channels * rows
    total = depth_len * channels * rows
    even = even_depth()

    @pl.when(even)
    def _():
        first_ref[...] = own_ref[total - part : total, :]
        second_ref[...] = own_ref[0:part, :]

    @pl.when(jnp.logical_not(even))
    def _():
        first_ref[...] = own_ref[0:part, :]
        second_ref[...] = own_ref[total - part : total, :]


def pack_fields(current_ref, previous_ref, forward_ref, first_ref, second_ref, *, steps):
    depth_len = current_ref.shape[1]
    up, down = steps + 1, steps

    def fill_bottom(out):
        out[0:up] = current_ref[0, depth_len - up : depth_len]
        out[up : 2 * up - 1] = previous_ref[0, depth_len - up + 1 : depth_len]
        for i in range(steps):
            out[2 * up - 1 + i] = forward_ref[i, 0, depth_len - 1].astype(jnp.float32)

    def fill_top(out):
        out[0:down] = current_ref[0, 0:down]
        out[down : 2 * down - 1] = previous_ref[0, 0 : down - 1]

    even = even_depth()

    @pl.when(even)
    def _():
        fill_bottom(first_ref)
        fill_top(second_ref)

    @pl.when(jnp.logical_not(even))
    def _():
        fill_top(first_ref)
        fill_bottom(second_ref)


def join_model(own_ref, first_ref, second_ref, out_ref, *, layer, depth_count):
    part = first_ref.shape[0]
    own = own_ref.shape[0]
    out_ref[part : part + own, :] = own_ref[...]
    even = even_depth()
    last = lax.axis_index("depth") == depth_count - 1

    @pl.when(even)
    def _():
        out_ref[0:part, :] = second_ref[...]
        out_ref[part + own : 2 * part + own, :] = first_ref[...]

    @pl.when(jnp.logical_not(even))
    def _():
        out_ref[0:part, :] = first_ref[...]
        out_ref[part + own : 2 * part + own, :] = second_ref[...]

    @pl.when(last)
    def _():
        out_ref[part + own : part + own + layer, :] = own_ref[own - layer : own, :]


def injection(assign_ref, residual_ref, receiver_ref, out_ref, *, steps, depth_len, rows):
    receivers = receiver_ref.shape[2]
    columns = out_ref.shape[3]
    count = out_ref.shape[1]
    geometry = assign_ref[lax.axis_index("shot")]
    first = lax.axis_index("depth") * depth_len - steps
    depth = receiver_ref[0, pl.ds(geometry, 1), :] - first
    flat = depth * rows + receiver_ref[1, pl.ds(geometry, 1), :]
    flat = jnp.where((depth >= 0) & (depth < count), flat, -1)
    cells = lax.broadcasted_iota(jnp.int32, (count * rows, receivers), 0)
    one_hot = jnp.where(cells == flat, 1.0, 0.0).astype(jnp.bfloat16)
    lanes = lax.broadcasted_iota(jnp.int32, (columns, receivers), 0)
    here = lanes == receiver_ref[2, pl.ds(geometry, 1), :]
    for i in range(steps):
        left = residual_ref[0, i : i + 1, :]
        total = None
        for _ in range(3):
            rounded = left.astype(jnp.bfloat16).astype(jnp.float32)
            left = left - rounded
            values = jnp.where(here, rounded, 0.0).astype(jnp.bfloat16)
            product = lax.dot_general(
                one_hot, values, (((1,), (1,)), ((), ())), preferred_element_type=jnp.float32
            )
            total = product if total is None else total + product
        out_ref[i] = total.reshape(count, rows, columns)


def march(
    assign_ref,
    source_ref,
    current_ref,
    previous_ref,
    forward_ref,
    first_ref,
    second_ref,
    added_ref,
    *refs,
    steps,
    shots,
    depth_count,
    channels,
    reach,
):
    gathered = refs[:shots]
    final_ref = refs[shots]
    chunks = refs[shots + 1 : 2 * shots + 1]
    blocks, coarse, even_rows, odd_rows, fields, across, bend, totals, result = refs[2 * shots + 1 :]
    depth_len, rows, columns = current_ref.shape[1:]
    up, down = steps + 1, steps
    height = up + depth_len + down
    depth_index = lax.axis_index("depth")
    shot_index = lax.axis_index("shot")
    is_even = depth_index % 2 == 0
    is_top = depth_index == 0
    is_last = depth_index == depth_count - 1
    coarse_rows = rows // 2
    share = coarse_rows // shots
    layers = depth_len // 2 + 2 * reach

    rim = jnp.zeros((height, PAD, columns), jnp.float32)
    for b in range(2):
        fields[b, :, 0:PAD, :] = rim
        fields[b, :, PAD + rows : 2 * PAD + rows, :] = rim
    across[:, 0:PAD, :] = rim
    across[:, PAD + rows : 2 * PAD + rows, :] = rim
    inner = slice(PAD, PAD + rows)
    fields[0, up : up + depth_len, inner, :] = current_ref[0]
    fields[1, up : up + depth_len, inner, :] = previous_ref[0]

    def from_above(ref):
        fields[0, 0:up, inner, :] = ref[0:up]
        fields[1, 1:up, inner, :] = ref[up : 2 * up - 1]
        for i in range(steps):
            result[i] = ref[2 * up - 1 + i]

    def from_below(ref):
        fields[0, up + depth_len : height, inner, :] = ref[0:down]
        fields[1, up + depth_len : height - 1, inner, :] = ref[down : 2 * down - 1]

    @pl.when(is_even)
    def _():
        from_above(second_ref)
        from_below(first_ref)

    @pl.when(jnp.logical_not(is_even))
    def _():
        from_above(first_ref)
        from_below(second_ref)

    @pl.when(is_top)
    def _():
        for b in range(2):
            fields[b, 0:up, inner, :] = jnp.zeros((up, rows, columns), jnp.float32)

    @pl.when(is_last)
    def _():
        for b in range(2):
            fields[b, up + depth_len : height, inner, :] = jnp.zeros(
                (down, rows, columns), jnp.float32
            )

    for j in range(shots):
        blocks[j] = gathered[j][...]
    for z in range(layers):
        for k in range(channels):
            at = (z * channels + k) * share
            for b in range(shots):
                coarse[z, k, b * share : (b + 1) * share, :] = blocks[shot_index ^ b, at : at + share, :]
            coarse[z, k, coarse_rows : coarse_rows + 1, :] = coarse[
                z, k, coarse_rows - 1 : coarse_rows, :
            ]
            scale = TIME_SQUARED if k < 3 else 0.25 * TIME_SQUARED
            here = coarse[z, k, 0:coarse_rows, :]
            after = coarse[z, k, 1 : coarse_rows + 1, :]
            even_rows[z, k, pl.ds(0, coarse_rows, stride=2), :] = here * scale
            even_rows[z, k, pl.ds(1, coarse_rows, stride=2), :] = (here + after) * (0.5 * scale)
    for z in range(layers - 1):
        for k in range(channels):
            odd_rows[z, k] = (even_rows[z, k] + even_rows[z + 1, k]) * 0.5

    lane = lax.broadcasted_iota(jnp.int32, (rows, columns), 1)
    leftmost = lane == 0
    rightmost = lane == columns - 1

    for i in range(steps):
        now, old = i % 2, 1 - i % 2
        lowest, highest = i, height - 1 - i
        for e in range(lowest, highest + 1):
            value = fields[now, e, inner, :]
            right = jnp.where(rightmost, 0.0, pltpu.roll(value, columns - 1, 1))
            left = jnp.where(leftmost, 0.0, pltpu.roll(value, 1, 1))
            across[e, inner, :] = right - left
            bend[e] = right + left - 2.0 * value
        for e in range(lowest + 1, highest):
            counted = up - 1 <= e < up + depth_len
            stepped = i < steps - 1 or up <= e < up + depth_len
            if not (counted or stepped):
                continue
            value = fields[now, e, inner, :]
            twice = 2.0 * value
            before = slice(PAD - 1, PAD - 1 + rows)
            after = slice(PAD + 1, PAD + 1 + rows)
            slopes = [
                fields[now, e + 1, inner, :] - twice + fields[now, e - 1, inner, :],
                fields[now, e, after, :] - twice + fields[now, e, before, :],
                bend[e],
                (fields[now, e + 1, after, :] - fields[now, e + 1, before, :])
                - (fields[now, e - 1, after, :] - fields[now, e - 1, before, :]),
                across[e + 1, inner, :] - across[e - 1, inner, :],
                across[e, after, :] - across[e, before, :],
            ]
            if counted:
                if e < up:
                    weight = result[i]
                else:
                    weight = forward_ref[i, 0, e - up].astype(jnp.float32)
                for k in range(channels):
                    if i == 0:
                        totals[k, e - up + 1] = weight * slopes[k]
                    else:
                        totals[k, e - up + 1] += weight * slopes[k]
            if stepped:
                z = e - up + 2 * reach
                table = even_rows if z % 2 == 0 else odd_rows
                change = table[z // 2, 0] * slopes[0]
                for k in range(1, channels):
                    change = change + table[z // 2, k] * slopes[k]
                updated = twice - fields[old, e, inner, :] + change + added_ref[i, e - 1]
                if e < up:
                    updated = jnp.where(is_top, 0.0, updated)
                if e >= up + depth_len:
                    updated = jnp.where(is_last, 0.0, updated)
                if i < steps - 1:
                    fields[old, e, inner, :] = updated
                else:
                    final_ref[0, e - up] = updated

    geometry = assign_ref[shot_index]
    first = depth_index * depth_len
    row = lax.broadcasted_iota(jnp.int32, (rows, columns), 0)
    near = (jnp.abs(row - source_ref[geometry, 1]) <= MUTE) & (
        jnp.abs(lane - source_ref[geometry, 2]) <= MUTE
    )
    near = jnp.where(near, 1, 0)
    masks = []
    for e in range(depth_len + 1):
        close = jnp.abs(first + e - 1 - source_ref[geometry, 0]) <= MUTE
        masks.append(near * jnp.where(close, 1, 0) > 0)
    rim_scale = jnp.where(is_top, 0.0, 0.5)
    last_scale = jnp.where(is_last, 1.0, 0.5)
    half = depth_len // 2
    for k in range(channels):
        kept = [jnp.where(masks[e], 0.0, totals[k, e]) for e in range(depth_len + 1)]
        for z in range(half):
            above = kept[0] * rim_scale if z == 0 else kept[2 * z] * 0.5
            below = kept[2 * z + 2] * (last_scale if z == half - 1 else 0.5)
            layer = kept[2 * z + 1] + above + below
            slot = steps + 1 + (k * half + z) % 4
            result[slot] = layer
            even = result[slot, pl.ds(0, coarse_rows, stride=2), :]
            odd = 0.5 * result[slot, pl.ds(1, coarse_rows, stride=2), :]
            across[0, PAD : PAD + coarse_rows, :] = odd
            line = lax.broadcasted_iota(jnp.int32, (coarse_rows, columns), 0)
            tail = jnp.where(line == coarse_rows - 1, odd, 0.0)
            value = even + odd + across[0, PAD - 1 : PAD - 1 + coarse_rows, :] + tail
            if k >= 3:
                value = value * 0.25
            at = (k * half + z) * share
            for b in range(shots):
                blocks[b, at : at + share, :] = value[b * share : (b + 1) * share, :]
    for j in range(shots):
        chunks[j][...] = blocks[shot_index ^ j, 0 : channels * half * share, :]


def finish(*refs, steps):
    parts, out_ref = refs[:-1], refs[-1]
    channels, depth_len, rows, columns = out_ref.shape
    total = parts[0][...]
    for part in parts[1:]:
        total = total + part[...]
    coarse = exact_dot(total, refine_matrix(columns), ((1,), (1,))) / steps
    for k in range(channels):
        for z in range(depth_len):
            at = (k * depth_len + z) * rows
            out_ref[k, z] = coarse[at : at + rows, :]


def on_device(
    forward, adjoint_last, adjoint_late, residuals, source_cells, receiver_cells, assignment, model
):
    steps = forward.shape[0]
    shots_here, depth_len, rows, columns = adjoint_last.shape
    channels, coarse_len, share, coarse_columns = model.shape
    shots = lax.axis_size("shot")
    depth_count = lax.axis_size("depth")
    reach = (steps + 1) // 2
    assert shots_here == 1 and depth_count % 2 == 0 and shots & (shots - 1) == 0
    assert depth_len > steps and coarse_len >= reach and share * shots * 2 == rows
    f32 = jnp.float32
    shape = lambda *dims: jax.ShapeDtypeStruct(dims, f32)
    call = lambda body, count, outs, **more: pl.pallas_call(
        body,
        in_specs=[VMEM] * count,
        out_specs=jax.tree.map(lambda _: VMEM, outs),
        out_shape=outs,
        **more,
    )
    first_pairs = [(i, i ^ 1) for i in range(depth_count)]
    second_pairs = [(i, (i + 1 if i % 2 else i - 1) % depth_count) for i in range(depth_count)]

    part = reach * channels * share
    own_rows = coarse_len * channels * share
    own, model_first, model_second = call(
        functools.partial(pack_model, reach=reach),
        1,
        (shape(own_rows, columns), shape(part, columns), shape(part, columns)),
        scratch_shapes=[pltpu.VMEM((own_rows, coarse_columns), f32)],
        name="pack_model",
    )(model)
    model_second = lax.ppermute(model_second, "depth", second_pairs)
    model_first = lax.ppermute(model_first, "depth", first_pairs)
    halo = 3 * steps + 1
    field_first, field_second = call(
        functools.partial(pack_fields, steps=steps),
        3,
        (shape(halo, rows, columns), shape(halo, rows, columns)),
        name="pack_fields",
    )(adjoint_last, adjoint_late, forward)
    field_second = lax.ppermute(field_second, "depth", second_pairs)
    field_first = lax.ppermute(field_first, "depth", first_pairs)
    joined_rows = own_rows + 2 * part
    joined = call(
        functools.partial(join_model, layer=channels * share, depth_count=depth_count),
        3,
        shape(joined_rows, columns),
        name="join_model",
    )(own, model_first, model_second)
    swap = lambda array, j: lax.ppermute(array, "shot", [(i, i ^ j) for i in range(shots)])
    gathered = [joined] + [swap(joined, j) for j in range(1, shots)]
    height = depth_len + 2 * steps + 1
    added = pl.pallas_call(
        functools.partial(injection, steps=steps, depth_len=depth_len, rows=rows),
        in_specs=[SMEM, VMEM, VMEM],
        out_specs=VMEM,
        out_shape=shape(steps, height - 2, rows, columns),
        name="injection",
    )(assignment, residuals, receiver_cells.transpose(2, 0, 1))
    layers = coarse_len + 2 * reach
    chunk = shape(channels * coarse_len * share, columns)
    final, *chunks = pl.pallas_call(
        functools.partial(
            march,
            steps=steps,
            shots=shots,
            depth_count=depth_count,
            channels=channels,
            reach=reach,
        ),
        in_specs=[SMEM, SMEM] + [VMEM] * (6 + shots),
        out_specs=[VMEM] * (1 + shots),
        out_shape=[shape(1, depth_len, rows, columns)] + [chunk] * shots,
        scratch_shapes=[
            pltpu.VMEM((shots, joined_rows, columns), f32),
            pltpu.VMEM((layers, channels, rows // 2 + PAD, columns), f32),
            pltpu.VMEM((layers, channels, rows, columns), f32),
            pltpu.VMEM((layers - 1, channels, rows, columns), f32),
            pltpu.VMEM((2, height, rows + 2 * PAD, columns), f32),
            pltpu.VMEM((height, rows + 2 * PAD, columns), f32),
            pltpu.VMEM((height, rows, columns), f32),
            pltpu.VMEM((channels, depth_len + 1, rows, columns), f32),
            pltpu.VMEM((steps + 5, rows, columns), f32),
        ],
        name="march",
    )(
        assignment,
        source_cells,
        adjoint_last,
        adjoint_late,
        forward,
        field_first,
        field_second,
        added,
        *gathered,
    )
    parts = [chunks[0]] + [swap(chunks[j], j) for j in range(1, shots)]
    gradients = call(
        functools.partial(finish, steps=steps), shots, shape(*model.shape), name="finish"
    )(*parts)
    return final, gradients


def solution(mesh):
    placed = (
        P(None, ("grp", "shot"), "depth", None, None),
        P(("grp", "shot"), "depth", None, None),
        P(("grp", "shot"), "depth", None, None),
        P(("grp", "shot"), None, None),
        P("grp", None),
        P("grp", None, None),
        P("grp"),
        P(None, ("grp", "depth"), "shot", None),
    )
    return jax.shard_map(
        on_device,
        mesh=mesh,
        in_specs=placed,
        out_specs=(
            P(("grp", "shot"), "depth", None, None),
            P(None, ("grp", "depth"), "shot", None),
        ),
        check_vma=False,
    )
```

time: 178 us -> 43.9 us (0.25)
  local copies, waits for them, and re-layouts: 52.1 us -> 2.65 us
  other arithmetic: 41.9 us -> 0 us
  waiting for transfers between devices: 37.2 us -> 14.8 us
  blocking collectives: 17.3 us -> 0 us
  between operations: 15.6 us -> 0.68 us
  Pallas kernels: 0 us -> 13.5 us
    unnamed x2 -> x0, waiting for transfers between devices: 37.1 us -> none
    all_gather x1 -> x0, blocking collectives: 17.3 us -> none  [on_device(): piece = lax.all_gather(extended, 'shot', axis=2, tiled=True)]
    slice x17 -> x0, local copies, waits for them, and re-layouts: 14.9 us -> none  [the longest x3 12.2 us: refine(): lax.slice_in_dim(coarse, coarse_count - 1, coarse_count, axis=dimension)]
    ppermute x5 -> x10, waiting for transfers between devices: 0.15 us -> 14.8 us  [the longest x6 10.1 us: on_device(): lax.ppermute(array, 'shot', [(i, i ^ j) for i in range(shots)])]
    pallas_call x0 -> x6, Pallas kernels: none -> 13.5 us  [the longest x1 4.17 us: on_device(): pl.pallas_call(functools.partial(march, steps=steps, shots=shots, depth_c...]
    mul x6 -> x0, other arithmetic: 12.5 us -> none  [the longest x1 10.7 us: refine(): (coarse + jnp.concatenate([later_rows, edge_row], axis=dimension)) * 0.5]
    another operation x6 -> x0, local copies, waits for them, and re-layouts: 10.8 us -> none  [the longest x2 10.8 us: refine(): merged = jnp.stack([coarse, middle], axis=dimension + 1)]
    scatter-add x4 -> x0, other arithmetic: 8.5 us -> none  [inject(): wave_field.reshape(-1).at[flat_index.reshape(-1)]]
  transfers between devices with their start and end apart: 6 -> 10, of which waited for: 2 -> 7; matrix products, arithmetic and copies ran while one was open for 35% -> 0% of each run, Pallas kernels for 0% -> 13%
where the time goes in v1:
time: 43.9 us; the launch traced here: 43.5 us
  waiting for transfers between devices  14.8 us (34%)
  Pallas kernels  13.5 us (31%)
  starting transfers between devices  11.9 us (27%)
  local copies, waits for them, and re-layouts  2.65 us (6%)
  between operations  0.68 us (2%)
    ppermute x6, waiting for transfers between devices, on_device(): lax.ppermute(array, 'shot', [(i, i ^ j) for i in range(shots)])  10.1 us
    ppermute x6, starting transfers between devices, on_device(): lax.ppermute(array, 'shot', [(i, i ^ j) for i in range(shots)])  8.77 us
    pallas_call x1, Pallas kernels, on_device(): pl.pallas_call(functools.partial(march, steps=steps, shots=shots, depth_c...  4.17 us
    ppermute x1, waiting for transfers between devices, on_device(): model_second = lax.ppermute(model_second, 'depth', second_pairs)  3.33 us
    unnamed x20, local copies, waits for them, and re-layouts  2.65 us
    pallas_call x1, Pallas kernels, on_device(): pl.pallas_call(functools.partial(injection, steps=steps, depth_len=depth_...  2.63 us
    ppermute x1, starting transfers between devices, on_device(): field_second = lax.ppermute(field_second, 'depth', second_pairs)  2.59 us
    pallas_call x1, Pallas kernels, on_device(): call(functools.partial(pack_fields, steps=steps), 3, (shape(halo, rows, c...  1.9 us
  transfers between devices with their start and end apart: 10, of which 7 were waited for; matrix products, arithmetic and copies ran while one was open for 0% of the time, Pallas kernels for 13%

profile of v1, /device:TPU:0, one launch (start us, length us, event | category | flops | bytes accessed | tf_op | source)
XLA Modules:
  0.0 43.5 jit_solution(396313637494289889)
XLA Ops:
  0.6 1.9 %pack_fields.1 = (f32[13,32,128]{2,1,0:T(8,128)}, f32[13,32,128]{2,1,0:T(8,128)}) custom-call(f32[1,8,32,128]{3,2,1,0:T(8,128)} %current_ref.3, f32[1,8,32,128]{3,2,1,0:T(8,128)} %previous_ref.3, bf16[4,1,8,32,128]{4,3,2,1,0:T(8,128)(2,1)} %forward_ref.3), custom_call_target="tpu_custom_call" | custom-call | tf_op jit(solution)/shard_map/pack_fields/pallas_call | solution.py:375
  2.5 0.5 %collective-permute-start = (f32[13,32,128]{2,1,0:T(8,128)}, f32[13,32,128]{2,1,0:T(8,128)S(1)}, u32[]{:S(2)}, u32[]{:S(2)}) collective-permute-start(f32[13,32,128]{2,1,0:T(8,128)} %get-tuple-element.12), channel_id=1, source_target_pairs={{0,4},{4,0},{8,12},{12,8},{1,5},{5,1},{9,13},{13,9},{2,6},{6,2},{1... | collective-permute-start | bytes 638984 | tf_op jit(solution)/shard_map/ppermute | solution.py:382
  3.0 2.6 %collective-permute-start.1 = (f32[13,32,128]{2,1,0:T(8,128)}, f32[13,32,128]{2,1,0:T(8,128)S(1)}, u32[]{:S(2)}, u32[]{:S(2)}) collective-permute-start(f32[13,32,128]{2,1,0:T(8,128)} %get-tuple-element.13), channel_id=1, source_target_pairs={{0,12},{4,8},{8,4},{12,0},{1,13},{5,9},{9,5},{13,1},{2,14},{6,10},... | collective-permute-start | bytes 638984 | tf_op jit(solution)/shard_map/ppermute | solution.py:381
  5.6 1.6 %pack_model.1 = (f32[96,128]{1,0:T(8,128)}, f32[48,128]{1,0:T(8,128)}, f32[48,128]{1,0:T(8,128)}) custom-call(f32[6,4,4,64]{3,2,1,0:T(4,128)} %model_ref.1), custom_call_target="tpu_custom_call" | custom-call | tf_op jit(solution)/shard_map/pack_model/pallas_call | solution.py:365
  7.2 0.0 collective-permute-start.2
  7.2 0.0 collective-permute-start.3
  7.2 1.4 %collective-permute-done.2.first_ref = f32[48,128]{1,0:T(8,128)S(1)} collective-permute-done((f32[48,128]{1,0:T(8,128)}, f32[48,128]{1,0:T(8,128)S(1)}, u32[]{:S(2)}, u32[]{:S(2)}) %collective-permute-start.2) | collective-permute-done | bytes 24608 | tf_op jit(solution)/shard_map/ppermute | solution.py:373
  8.6 0.0 copy-start.8
  8.6 3.3 %collective-permute-done.3.second_ref = f32[48,128]{1,0:T(8,128)S(1)} collective-permute-done((f32[48,128]{1,0:T(8,128)}, f32[48,128]{1,0:T(8,128)S(1)}, u32[]{:S(2)}, u32[]{:S(2)}) %collective-permute-start.3) | collective-permute-done | bytes 24608 | tf_op jit(solution)/shard_map/ppermute | solution.py:372
  12.0 0.0 copy-start.9
  12.0 0.0 copy-done.8
  12.0 0.6 %copy-done.9 = f32[48,128]{1,0:T(8,128)} copy-done((f32[48,128]{1,0:T(8,128)}, f32[48,128]{1,0:T(8,128)S(1)}, u32[]{:S(2)}) %copy-start.9) | copy-done | bytes 24600
  12.6 1.5 %join_model.1.refs_0_ = f32[192,128]{1,0:T(8,128)} custom-call(f32[96,128]{1,0:T(8,128)} %get-tuple-element.14.own_ref, f32[48,128]{1,0:T(8,128)} %copy-done.8, f32[48,128]{1,0:T(8,128)} %copy-done.9), custom_call_target="tpu_custom_call" | custom-call | tf_op jit(solution)/shard_map/join_model/pallas_call | solution.py:384
  14.0 3.2 %collective-permute-start.6 = (f32[192,128]{1,0:T(8,128)}, f32[192,128]{1,0:T(8,128)S(1)}, u32[]{:S(2)}, u32[]{:S(2)}) collective-permute-start(f32[192,128]{1,0:T(8,128)} %join_model.1.refs_0_), channel_id=1, source_target_pairs={{0,3},{1,2},{2,1},{3,0},{4,7},{5,6},{6,5},{7,4},{8,11},{9,10},{10,... | collective-permute-start | bytes 294920 | tf_op jit(solution)/shard_map/ppermute | solution.py:390
  17.3 0.0 collective-permute-start.5
  17.3 1.1 %collective-permute-start.4 = (f32[192,128]{1,0:T(8,128)}, f32[192,128]{1,0:T(8,128)S(1)}, u32[]{:S(2)}, u32[]{:S(2)}) collective-permute-start(f32[192,128]{1,0:T(8,128)} %join_model.1.refs_0_), channel_id=1, source_target_pairs={{0,1},{1,0},{2,3},{3,2},{4,5},{5,4},{6,7},{7,6},{8,9},{9,8},{10,11... | collective-permute-start | bytes 294920 | tf_op jit(solution)/shard_map/ppermute | solution.py:390
  18.4 2.6 %injection.1.added_ref = f32[4,15,32,128]{3,2,1,0:T(8,128)} custom-call(s32[4]{0:T(128)} %assign_ref.3, f32[1,4,256]{2,1,0:T(4,128)} %residual_ref.1, s32[3,4,256]{2,1,0:T(4,128)} %bitcast.1), custom_call_target="tpu_custom_call" | custom-call | tf_op jit(solution)/shard_map/injection/pallas_call | solution.py:393
  21.1 0.8 %collective-permute-done.6.refs_3_ = f32[192,128]{1,0:T(8,128)S(1)} collective-permute-done((f32[192,128]{1,0:T(8,128)}, f32[192,128]{1,0:T(8,128)S(1)}, u32[]{:S(2)}, u32[]{:S(2)}) %collective-permute-start.6) | collective-permute-done | bytes 98336 | tf_op jit(solution)/shard_map/ppermute | solution.py:390
  21.8 0.0 copy-start.2
  21.8 4.6 %collective-permute-done.5.refs_2_ = f32[192,128]{1,0:T(8,128)S(1)} collective-permute-done((f32[192,128]{1,0:T(8,128)}, f32[192,128]{1,0:T(8,128)S(1)}, u32[]{:S(2)}, u32[]{:S(2)}) %collective-permute-start.5) | collective-permute-done | bytes 98336 | tf_op jit(solution)/shard_map/ppermute | solution.py:390
  26.4 0.0 copy-start.3
  26.4 0.0 collective-permute-done.4.refs_1_
  26.4 0.0 copy-start.4
  26.4 0.0 collective-permute-done.first_ref
  26.5 0.0 copy-start
  26.5 0.0 collective-permute-done.1.second_ref
  26.5 0.0 copy-done.2
  26.5 0.6 %copy-done.3 = f32[192,128]{1,0:T(8,128)} copy-done((f32[192,128]{1,0:T(8,128)}, f32[192,128]{1,0:T(8,128)S(1)}, u32[]{:S(2)}) %copy-start.3) | copy-done | bytes 98328
  27.1 0.0 copy-done.4
  27.1 0.1 copy-done
  27.2 0.0 copy-start.1
  27.2 0.7 %copy-done.1 = f32[13,32,128]{2,1,0:T(8,128)} copy-done((f32[13,32,128]{2,1,0:T(8,128)}, f32[13,32,128]{2,1,0:T(8,128)S(1)}, u32[]{:S(2)}) %copy-start.1) | copy-done | bytes 213016
  27.9 4.2 %march.1 = (f32[1,8,32,128]{3,2,1,0:T(8,128)}, f32[96,128]{1,0:T(8,128)}, f32[96,128]{1,0:T(8,128)}, f32[96,128]{1,0:T(8,128)}, f32[96,128]{1,0:T(8,128)}) custom-call(s32[4]{0:T(128)} %assign_ref.3, s32[4,3]{1,0:T(4,128)} %source_ref.1, f32[1,8,32,128]{3,2,1,0:T(8,128)} %current_ref.3, f32[1,8,32,128]{3,2,1,0:T(8,128)} %previous_ref.3, ...), custom_call_target="tpu_custom_call" | custom-call | tf_op jit(solution)/shard_map/march/pallas_call | solution.py:402
  32.1 0.5 %collective-permute-start.7 = (f32[96,128]{1,0:T(8,128)}, f32[96,128]{1,0:T(8,128)S(1)}, u32[]{:S(2)}, u32[]{:S(2)}) collective-permute-start(f32[96,128]{1,0:T(8,128)} %get-tuple-element.19), channel_id=1, source_target_pairs={{0,1},{1,0},{2,3},{3,2},{4,5},{5,4},{6,7},{7,6},{8,9},{9,8},{10,11... | collective-permute-start | bytes 147464 | tf_op jit(solution)/shard_map/ppermute | solution.py:390
  32.6 2.5 %collective-permute-start.8 = (f32[96,128]{1,0:T(8,128)}, f32[96,128]{1,0:T(8,128)S(1)}, u32[]{:S(2)}, u32[]{:S(2)}) collective-permute-start(f32[96,128]{1,0:T(8,128)} %get-tuple-element.20), channel_id=1, source_target_pairs={{0,2},{1,3},{2,0},{3,1},{4,6},{5,7},{6,4},{7,5},{8,10},{9,11},{10,... | collective-permute-start | bytes 147464 | tf_op jit(solution)/shard_map/ppermute | solution.py:390
  35.1 1.3 %collective-permute-start.9 = (f32[96,128]{1,0:T(8,128)}, f32[96,128]{1,0:T(8,128)S(1)}, u32[]{:S(2)}, u32[]{:S(2)}) collective-permute-start(f32[96,128]{1,0:T(8,128)} %get-tuple-element.21), channel_id=1, source_target_pairs={{0,3},{1,2},{2,1},{3,0},{4,7},{5,6},{6,5},{7,4},{8,11},{9,10},{10,... | collective-permute-start | bytes 147464 | tf_op jit(solution)/shard_map/ppermute | solution.py:390
  36.5 0.2 collective-permute-done.7.refs_1_
  36.7 0.0 copy-start.5
  36.7 1.6 %collective-permute-done.8.refs_2_ = f32[96,128]{1,0:T(8,128)S(1)} collective-permute-done((f32[96,128]{1,0:T(8,128)}, f32[96,128]{1,0:T(8,128)S(1)}, u32[]{:S(2)}, u32[]{:S(2)}) %collective-permute-start.8) | collective-permute-done | bytes 49184 | tf_op jit(solution)/shard_map/ppermute | solution.py:390
  38.3 0.0 copy-start.6
  38.3 2.9 %collective-permute-done.9.refs_3_ = f32[96,128]{1,0:T(8,128)S(1)} collective-permute-done((f32[96,128]{1,0:T(8,128)}, f32[96,128]{1,0:T(8,128)S(1)}, u32[]{:S(2)}, u32[]{:S(2)}) %collective-permute-start.9) | collective-permute-done | bytes 49184 | tf_op jit(solution)/shard_map/ppermute | solution.py:390
  41.2 0.0 copy-start.7
  41.2 0.0 copy-done.5
  41.2 0.0 copy-done.6
  41.2 0.6 %copy-done.7 = f32[96,128]{1,0:T(8,128)} copy-done((f32[96,128]{1,0:T(8,128)}, f32[96,128]{1,0:T(8,128)S(1)}, u32[]{:S(2)}) %copy-start.7) | copy-done | bytes 49176
  41.8 1.7 %finish.1 = f32[6,4,4,64]{3,2,1,0:T(4,128)} custom-call(f32[96,128]{1,0:T(8,128)} %get-tuple-element.18.refs_0_, f32[96,128]{1,0:T(8,128)} %copy-done.5, f32[96,128]{1,0:T(8,128)} %copy-done.6, f32[96,128]{1,0:T(8,128)} %copy-done.7), custom_call_target="tpu_custom_call" | custom-call | tf_op jit(solution)/shard_map/finish/pallas_call | solution.py:438
Async XLA Ops:
  2.5 23.9 %collective-permute-start = (f32[13,32,128]{2,1,0:T(8,128)}, f32[13,32,128]{2,1,0:T(8,128)S(1)}, u32[]{:S(2)}, u32[]{:S(2)}) collective-permute-start(f32[13,32,128]{2,1,0:T(8,128)} %get-tuple-element.12), channel_id=1, source_target_pairs={{0,4},{4,0},{8,12},{12,8},{1,5},{5,1},{9,13},{13,9},{2,6},{6,2},{1... | collective-permute-start | bytes 638984 | tf_op jit(solution)/shard_map/ppermute | solution.py:382
  3.0 23.4 %collective-permute-start.1 = (f32[13,32,128]{2,1,0:T(8,128)}, f32[13,32,128]{2,1,0:T(8,128)S(1)}, u32[]{:S(2)}, u32[]{:S(2)}) collective-permute-start(f32[13,32,128]{2,1,0:T(8,128)} %get-tuple-element.13), channel_id=1, source_target_pairs={{0,12},{4,8},{8,4},{12,0},{1,13},{5,9},{9,5},{13,1},{2,14},{6,10},... | collective-permute-start | bytes 638984 | tf_op jit(solution)/shard_map/ppermute | solution.py:381
  7.2 1.4 %collective-permute-start.2 = (f32[48,128]{1,0:T(8,128)}, f32[48,128]{1,0:T(8,128)S(1)}, u32[]{:S(2)}, u32[]{:S(2)}) collective-permute-start(f32[48,128]{1,0:T(8,128)} %get-tuple-element.15), channel_id=1, source_target_pairs={{0,4},{4,0},{8,12},{12,8},{1,5},{5,1},{9,13},{13,9},{2,6},{6,2},{1... | collective-permute-start | bytes 73736 | tf_op jit(solution)/shard_map/ppermute | solution.py:373
  7.2 4.7 %collective-permute-start.3 = (f32[48,128]{1,0:T(8,128)}, f32[48,128]{1,0:T(8,128)S(1)}, u32[]{:S(2)}, u32[]{:S(2)}) collective-permute-start(f32[48,128]{1,0:T(8,128)} %get-tuple-element.16), channel_id=1, source_target_pairs={{0,12},{4,8},{8,4},{12,0},{1,13},{5,9},{9,5},{13,1},{2,14},{6,10},... | collective-permute-start | bytes 73736 | tf_op jit(solution)/shard_map/ppermute | solution.py:372
  8.6 3.3 %copy-start.8 = (f32[48,128]{1,0:T(8,128)}, f32[48,128]{1,0:T(8,128)S(1)}, u32[]{:S(2)}) copy-start(f32[48,128]{1,0:T(8,128)S(1)} %collective-permute-done.2.first_ref) | copy-start | bytes 73732
  12.0 0.6 %copy-start.9 = (f32[48,128]{1,0:T(8,128)}, f32[48,128]{1,0:T(8,128)S(1)}, u32[]{:S(2)}) copy-start(f32[48,128]{1,0:T(8,128)S(1)} %collective-permute-done.3.second_ref) | copy-start | bytes 73732
  14.0 7.8 %collective-permute-start.6 = (f32[192,128]{1,0:T(8,128)}, f32[192,128]{1,0:T(8,128)S(1)}, u32[]{:S(2)}, u32[]{:S(2)}) collective-permute-start(f32[192,128]{1,0:T(8,128)} %join_model.1.refs_0_), channel_id=1, source_target_pairs={{0,3},{1,2},{2,1},{3,0},{4,7},{5,6},{6,5},{7,4},{8,11},{9,10},{10,... | collective-permute-start | bytes 294920 | tf_op jit(solution)/shard_map/ppermute | solution.py:390
  17.3 9.2 %collective-permute-start.5 = (f32[192,128]{1,0:T(8,128)}, f32[192,128]{1,0:T(8,128)S(1)}, u32[]{:S(2)}, u32[]{:S(2)}) collective-permute-start(f32[192,128]{1,0:T(8,128)} %join_model.1.refs_0_), channel_id=1, source_target_pairs={{0,2},{1,3},{2,0},{3,1},{4,6},{5,7},{6,4},{7,5},{8,10},{9,11},{10,... | collective-permute-start | bytes 294920 | tf_op jit(solution)/shard_map/ppermute | solution.py:390
  17.3 9.2 %collective-permute-start.4 = (f32[192,128]{1,0:T(8,128)}, f32[192,128]{1,0:T(8,128)S(1)}, u32[]{:S(2)}, u32[]{:S(2)}) collective-permute-start(f32[192,128]{1,0:T(8,128)} %join_model.1.refs_0_), channel_id=1, source_target_pairs={{0,1},{1,0},{2,3},{3,2},{4,5},{5,4},{6,7},{7,6},{8,9},{9,8},{10,11... | collective-permute-start | bytes 294920 | tf_op jit(solution)/shard_map/ppermute | solution.py:390
  21.8 4.6 %copy-start.2 = (f32[192,128]{1,0:T(8,128)}, f32[192,128]{1,0:T(8,128)S(1)}, u32[]{:S(2)}) copy-start(f32[192,128]{1,0:T(8,128)S(1)} %collective-permute-done.6.refs_3_) | copy-start | bytes 294916
  26.4 0.7 %copy-start.3 = (f32[192,128]{1,0:T(8,128)}, f32[192,128]{1,0:T(8,128)S(1)}, u32[]{:S(2)}) copy-start(f32[192,128]{1,0:T(8,128)S(1)} %collective-permute-done.5.refs_2_) | copy-start | bytes 294916
  26.4 0.7 %copy-start.4 = (f32[192,128]{1,0:T(8,128)}, f32[192,128]{1,0:T(8,128)S(1)}, u32[]{:S(2)}) copy-start(f32[192,128]{1,0:T(8,128)S(1)} %collective-permute-done.4.refs_1_) | copy-start | bytes 294916
  26.5 0.8 %copy-start = (f32[13,32,128]{2,1,0:T(8,128)}, f32[13,32,128]{2,1,0:T(8,128)S(1)}, u32[]{:S(2)}) copy-start(f32[13,32,128]{2,1,0:T(8,128)S(1)} %collective-permute-done.first_ref) | copy-start | bytes 638980
  27.2 0.7 %copy-start.1 = (f32[13,32,128]{2,1,0:T(8,128)}, f32[13,32,128]{2,1,0:T(8,128)S(1)}, u32[]{:S(2)}) copy-start(f32[13,32,128]{2,1,0:T(8,128)S(1)} %collective-permute-done.1.second_ref) | copy-start | bytes 638980
  32.1 4.6 %collective-permute-start.7 = (f32[96,128]{1,0:T(8,128)}, f32[96,128]{1,0:T(8,128)S(1)}, u32[]{:S(2)}, u32[]{:S(2)}) collective-permute-start(f32[96,128]{1,0:T(8,128)} %get-tuple-element.19), channel_id=1, source_target_pairs={{0,1},{1,0},{2,3},{3,2},{4,5},{5,4},{6,7},{7,6},{8,9},{9,8},{10,11... | collective-permute-start | bytes 147464 | tf_op jit(solution)/shard_map/ppermute | solution.py:390
  32.6 5.7 %collective-permute-start.8 = (f32[96,128]{1,0:T(8,128)}, f32[96,128]{1,0:T(8,128)S(1)}, u32[]{:S(2)}, u32[]{:S(2)}) collective-permute-start(f32[96,128]{1,0:T(8,128)} %get-tuple-element.20), channel_id=1, source_target_pairs={{0,2},{1,3},{2,0},{3,1},{4,6},{5,7},{6,4},{7,5},{8,10},{9,11},{10,... | collective-permute-start | bytes 147464 | tf_op jit(solution)/shard_map/ppermute | solution.py:390
  35.1 6.1 %collective-permute-start.9 = (f32[96,128]{1,0:T(8,128)}, f32[96,128]{1,0:T(8,128)S(1)}, u32[]{:S(2)}, u32[]{:S(2)}) collective-permute-start(f32[96,128]{1,0:T(8,128)} %get-tuple-element.21), channel_id=1, source_target_pairs={{0,3},{1,2},{2,1},{3,0},{4,7},{5,6},{6,5},{7,4},{8,11},{9,10},{10,... | collective-permute-start | bytes 147464 | tf_op jit(solution)/shard_map/ppermute | solution.py:390
  36.7 4.5 %copy-start.5 = (f32[96,128]{1,0:T(8,128)}, f32[96,128]{1,0:T(8,128)S(1)}, u32[]{:S(2)}) copy-start(f32[96,128]{1,0:T(8,128)S(1)} %collective-permute-done.7.refs_1_) | copy-start | bytes 147460
  38.3 2.9 %copy-start.6 = (f32[96,128]{1,0:T(8,128)}, f32[96,128]{1,0:T(8,128)S(1)}, u32[]{:S(2)}) copy-start(f32[96,128]{1,0:T(8,128)S(1)} %collective-permute-done.8.refs_2_) | copy-start | bytes 147460
  41.2 0.6 %copy-start.7 = (f32[96,128]{1,0:T(8,128)}, f32[96,128]{1,0:T(8,128)S(1)}, u32[]{:S(2)}) copy-start(f32[96,128]{1,0:T(8,128)S(1)} %collective-permute-done.9.refs_3_) | copy-start | bytes 147460

commit v2 on v1

v2 whole, which is shorter than its diff:
```python
import functools

import jax
import jax.numpy as jnp
from jax import lax
from jax.experimental import pallas as pl
from jax.experimental.pallas import tpu as pltpu
from jax.sharding import PartitionSpec as P

MUTE = 3
TIME_SQUARED = 0.2
PAD = 8
VMEM = pl.BlockSpec(memory_space=pltpu.VMEM)
SMEM = pl.BlockSpec(memory_space=pltpu.SMEM)
HBM = pl.BlockSpec(memory_space=pltpu.HBM)
LIMIT = pltpu.CompilerParams(vmem_limit_bytes=16 * 1024 * 1024)


def refine_matrix(coarse):
    row = lax.broadcasted_iota(jnp.int32, (coarse, 2 * coarse), 0)
    column = lax.broadcasted_iota(jnp.int32, (coarse, 2 * coarse), 1)
    here = column // 2
    after = jnp.minimum(here + 1, coarse - 1)
    odd = (column % 2) == 1
    at_here = jnp.where(row == here, 1.0, 0.0)
    at_after = jnp.where(row == after, 1.0, 0.0)
    return jnp.where(odd, 0.5 * (at_here + at_after), at_here).astype(jnp.float32)


def exact_dot(left, right, contract):
    return lax.dot_general(
        left,
        right,
        (contract, ((), ())),
        precision=lax.Precision.HIGHEST,
        preferred_element_type=jnp.float32,
    )


def even_depth():
    return lax.axis_index("depth") % 2 == 0


def pack(
    model_ref,
    current_ref,
    previous_ref,
    forward_ref,
    own_ref,
    model_first,
    model_second,
    field_first,
    field_second,
    block,
    staged,
    weights,
    sems,
    *,
    steps,
    reach,
):
    channels, coarse_len, rows, coarse_columns = block.shape
    depth_len = current_ref.shape[1]
    up, down = steps + 1, steps
    even = even_depth()
    model_copy = pltpu.make_async_copy(model_ref, block, sems.at[0])
    weight_copy = pltpu.make_async_copy(
        forward_ref.at[:, 0, depth_len - 1], weights, sems.at[1]
    )
    model_copy.start()
    weight_copy.start()

    def copies(bottom, top):
        return [
            pltpu.make_async_copy(
                current_ref.at[0, depth_len - up : depth_len], bottom.at[0:up], sems.at[2]
            ),
            pltpu.make_async_copy(
                previous_ref.at[0, depth_len - up + 1 : depth_len],
                bottom.at[up : 2 * up - 1],
                sems.at[3],
            ),
            pltpu.make_async_copy(current_ref.at[0, 0:down], top.at[0:down], sems.at[4]),
            pltpu.make_async_copy(
                previous_ref.at[0, 0 : down - 1], top.at[down : 2 * down - 1], sems.at[5]
            ),
        ]

    @pl.when(even)
    def _():
        for copy in copies(field_first, field_second):
            copy.start()

    @pl.when(jnp.logical_not(even))
    def _():
        for copy in copies(field_second, field_first):
            copy.start()

    model_copy.wait()
    for z in range(coarse_len):
        for k in range(channels):
            at = (z * channels + k) * rows
            staged[at : at + rows, :] = block[k, z]
    own_ref[...] = exact_dot(staged[...], refine_matrix(coarse_columns), ((1,), (0,)))
    part = reach * channels * rows
    total = coarse_len * channels * rows
    weight_copy.wait()

    @pl.when(even)
    def _():
        model_first[...] = own_ref[total - part : total, :]
        model_second[...] = own_ref[0:part, :]
        for i in range(steps):
            field_first[2 * up - 1 + i] = weights[i].astype(jnp.float32)
        for copy in copies(field_first, field_second):
            copy.wait()

    @pl.when(jnp.logical_not(even))
    def _():
        model_first[...] = own_ref[0:part, :]
        model_second[...] = own_ref[total - part : total, :]
        for i in range(steps):
            field_second[2 * up - 1 + i] = weights[i].astype(jnp.float32)
        for copy in copies(field_second, field_first):
            copy.wait()


def join_model(own_ref, first_ref, second_ref, out_ref, *, layer, depth_count):
    part = first_ref.shape[0]
    own = own_ref.shape[0]
    out_ref[part : part + own, :] = own_ref[...]
    even = even_depth()
    last = lax.axis_index("depth") == depth_count - 1

    @pl.when(even)
    def _():
        out_ref[0:part, :] = second_ref[...]
        out_ref[part + own : 2 * part + own, :] = first_ref[...]

    @pl.when(jnp.logical_not(even))
    def _():
        out_ref[0:part, :] = first_ref[...]
        out_ref[part + own : 2 * part + own, :] = second_ref[...]

    @pl.when(last)
    def _():
        out_ref[part + own : part + own + layer, :] = own_ref[own - layer : own, :]


def injection(assign_ref, residual_ref, receiver_ref, out_ref, *, steps, depth_len, rows):
    receivers = receiver_ref.shape[2]
    columns = out_ref.shape[3]
    count = out_ref.shape[1]
    geometry = assign_ref[lax.axis_index("shot")]
    first = lax.axis_index("depth") * depth_len - steps
    depth = receiver_ref[0, pl.ds(geometry, 1), :] - first
    flat = depth * rows + receiver_ref[1, pl.ds(geometry, 1), :]
    flat = jnp.where((depth >= 0) & (depth < count), flat, -1)
    cells = lax.broadcasted_iota(jnp.int32, (count * rows, receivers), 0)
    one_hot = jnp.where(cells == flat, 1.0, 0.0).astype(jnp.bfloat16)
    lanes = lax.broadcasted_iota(jnp.int32, (columns, receivers), 0)
    here = lanes == receiver_ref[2, pl.ds(geometry, 1), :]
    for i in range(steps):
        left = residual_ref[0, i : i + 1, :]
        total = None
        for _ in range(3):
            rounded = left.astype(jnp.bfloat16).astype(jnp.float32)
            left = left - rounded
            values = jnp.where(here, rounded, 0.0).astype(jnp.bfloat16)
            product = lax.dot_general(
                one_hot, values, (((1,), (1,)), ((), ())), preferred_element_type=jnp.float32
            )
            total = product if total is None else total + product
        out_ref[i] = total.reshape(count, rows, columns)


def slopes_at(field, across, bend, e, rows):
    inner = slice(PAD, PAD + rows)
    before = slice(PAD - 1, PAD - 1 + rows)
    after = slice(PAD + 1, PAD + 1 + rows)
    twice = 2.0 * field[e, inner, :]
    slopes = [
        field[e + 1, inner, :] - twice + field[e - 1, inner, :],
        field[e, after, :] - twice + field[e, before, :],
        bend[e],
        (field[e + 1, after, :] - field[e + 1, before, :])
        - (field[e - 1, after, :] - field[e - 1, before, :]),
        across[e + 1, inner, :] - across[e - 1, inner, :],
        across[e, after, :] - across[e, before, :],
    ]
    return twice, slopes


def columns_of(field, across, bend, lowest, highest, rows):
    columns = field.shape[2]
    inner = slice(PAD, PAD + rows)
    lane = lax.broadcasted_iota(jnp.int32, (rows, columns), 1)
    for e in range(lowest, highest + 1):
        value = field[e, inner, :]
        right = jnp.where(lane == columns - 1, 0.0, pltpu.roll(value, columns - 1, 1))
        left = jnp.where(lane == 0, 0.0, pltpu.roll(value, 1, 1))
        across[e, inner, :] = right - left
        bend[e] = right + left - 2.0 * value


def clear_rim(field, rows):
    height, _, columns = field.shape
    rim = jnp.zeros((height, PAD, columns), jnp.float32)
    field[:, 0:PAD, :] = rim
    field[:, PAD + rows : 2 * PAD + rows, :] = rim


def prepare(
    current_ref,
    previous_ref,
    forward_ref,
    first_ref,
    second_ref,
    added_ref,
    field,
    start_slopes,
    start_base,
    start_totals,
    weights,
    across,
    bend,
    older,
    *,
    steps,
    depth_count,
):
    depth_len, rows, _ = current_ref.shape[1:]
    up, down = steps + 1, steps
    height = up + depth_len + down
    depth_index = lax.axis_index("depth")
    is_even = depth_index % 2 == 0
    inner = slice(PAD, PAD + rows)
    clear_rim(field, rows)
    clear_rim(across, rows)
    field[up : up + depth_len, inner, :] = current_ref[0]
    older[up : up + depth_len] = previous_ref[0]
    for i in range(steps):
        weights[i, 1 : depth_len + 1] = forward_ref[i, 0].astype(jnp.float32)

    def from_above(ref):
        field[0:up, inner, :] = ref[0:up]
        older[1:up] = ref[up : 2 * up - 1]
        for i in range(steps):
            weights[i, 0] = ref[2 * up - 1 + i]

    def from_below(ref):
        field[up + depth_len : height, inner, :] = ref[0:down]
        older[up + depth_len : height - 1] = ref[down : 2 * down - 1]

    @pl.when(is_even)
    def _():
        from_above(second_ref)
        from_below(first_ref)

    @pl.when(jnp.logical_not(is_even))
    def _():
        from_above(first_ref)
        from_below(second_ref)

    @pl.when(depth_index == 0)
    def _():
        field[0:up, inner, :] = jnp.zeros((up,) + current_ref.shape[2:], jnp.float32)
        older[0:up] = jnp.zeros((up,) + current_ref.shape[2:], jnp.float32)

    @pl.when(depth_index == depth_count - 1)
    def _():
        field[up + depth_len : height, inner, :] = jnp.zeros(
            (down,) + current_ref.shape[2:], jnp.float32
        )
        older[up + depth_len : height] = jnp.zeros((down,) + current_ref.shape[2:], jnp.float32)

    columns_of(field, across, bend, 0, height - 1, rows)
    for e in range(1, height - 1):
        twice, slopes = slopes_at(field, across, bend, e, rows)
        for k, slope in enumerate(slopes):
            start_slopes[k, e - 1] = slope
            if up - 1 <= e < up + depth_len:
                start_totals[k, e - up + 1] = weights[0, e - up + 1] * slope
        start_base[e - 1] = twice - older[e] + added_ref[0, e - 1]


def march(
    assign_ref,
    source_ref,
    field,
    start_slopes,
    start_base,
    start_totals,
    weights,
    added_ref,
    *refs,
    steps,
    shots,
    depth_count,
    reach,
):
    gathered = refs[:shots]
    final_ref = refs[shots]
    chunks = refs[shots + 1 : 2 * shots + 1]
    blocks, coarse, even_rows, odd_rows, ones, twos, across, bend, totals, result = refs[
        2 * shots + 1 :
    ]
    depth_len, rows, columns = final_ref.shape[1:]
    channels = start_slopes.shape[0]
    up, down = steps + 1, steps
    height = up + depth_len + down
    depth_index = lax.axis_index("depth")
    shot_index = lax.axis_index("shot")
    is_top = depth_index == 0
    is_last = depth_index == depth_count - 1
    coarse_rows = rows // 2
    share = coarse_rows // shots
    layers = depth_len // 2 + 2 * reach
    inner = slice(PAD, PAD + rows)
    for scratch in (ones, twos, across):
        clear_rim(scratch, rows)

    for j in range(shots):
        blocks[j] = gathered[j][...]
    for z in range(layers):
        for k in range(channels):
            at = (z * channels + k) * share
            for b in range(shots):
                coarse[z, k, b * share : (b + 1) * share, :] = blocks[
                    shot_index ^ b, at : at + share, :
                ]
            coarse[z, k, coarse_rows : coarse_rows + 1, :] = coarse[
                z, k, coarse_rows - 1 : coarse_rows, :
            ]
            scale = TIME_SQUARED if k < 3 else 0.25 * TIME_SQUARED
            here = coarse[z, k, 0:coarse_rows, :]
            after = coarse[z, k, 1 : coarse_rows + 1, :]
            even_rows[z, k, pl.ds(0, coarse_rows, stride=2), :] = here * scale
            even_rows[z, k, pl.ds(1, coarse_rows, stride=2), :] = (here + after) * (0.5 * scale)
    for z in range(layers - 1):
        for k in range(channels):
            odd_rows[z, k] = (even_rows[z, k] + even_rows[z + 1, k]) * 0.5

    for i in range(steps):
        now = field if i == 0 else (ones if i % 2 else twos)
        old = field if i == 1 else (twos if i % 2 else ones)
        new = twos if i % 2 else ones
        if i > 0:
            columns_of(now, across, bend, i, height - 1 - i, rows)
        for e in range(i + 1, height - 1 - i):
            counted = up - 1 <= e < up + depth_len and i > 0
            stepped = i < steps - 1 or up <= e < up + depth_len
            if not (counted or stepped):
                continue
            if i == 0:
                slopes = [start_slopes[k, e - 1] for k in range(channels)]
                base = start_base[e - 1]
            else:
                twice, slopes = slopes_at(now, across, bend, e, rows)
            if counted:
                weight = weights[i, e - up + 1]
                for k in range(channels):
                    so_far = start_totals if i == 1 else totals
                    totals[k, e - up + 1] = so_far[k, e - up + 1] + weight * slopes[k]
            if stepped:
                if i > 0:
                    base = twice - old[e, inner, :] + added_ref[i, e - 1]
                z = e - up + 2 * reach
                table = even_rows if z % 2 == 0 else odd_rows
                change = table[z // 2, 0] * slopes[0]
                for k in range(1, channels):
                    change = change + table[z // 2, k] * slopes[k]
                updated = base + change
                if e < up:
                    updated = jnp.where(is_top, 0.0, updated)
                if e >= up + depth_len:
                    updated = jnp.where(is_last, 0.0, updated)
                if i < steps - 1:
                    new[e, inner, :] = updated
                else:
                    final_ref[0, e - up] = updated
    if steps == 1:
        totals[...] = start_totals[...]

    geometry = assign_ref[shot_index]
    first = depth_index * depth_len
    row = lax.broadcasted_iota(jnp.int32, (rows, columns), 0)
    lane = lax.broadcasted_iota(jnp.int32, (rows, columns), 1)
    near = (jnp.abs(row - source_ref[geometry, 1]) <= MUTE) & (
        jnp.abs(lane - source_ref[geometry, 2]) <= MUTE
    )
    near = jnp.where(near, 1, 0)
    masks = []
    for e in range(depth_len + 1):
        close = jnp.abs(first + e - 1 - source_ref[geometry, 0]) <= MUTE
        masks.append(near * jnp.where(close, 1, 0) > 0)
    rim_scale = jnp.where(is_top, 0.0, 0.5)
    last_scale = jnp.where(is_last, 1.0, 0.5)
    half = depth_len // 2
    line = lax.broadcasted_iota(jnp.int32, (coarse_rows, columns), 0)
    for k in range(channels):
        kept = [jnp.where(masks[e], 0.0, totals[k, e]) for e in range(depth_len + 1)]
        for z in range(half):
            above = kept[0] * rim_scale if z == 0 else kept[2 * z] * 0.5
            below = kept[2 * z + 2] * (last_scale if z == half - 1 else 0.5)
            slot = (k * half + z) % result.shape[0]
            result[slot] = kept[2 * z + 1] + above + below
            even = result[slot, pl.ds(0, coarse_rows, stride=2), :]
            odd = 0.5 * result[slot, pl.ds(1, coarse_rows, stride=2), :]
            ones[slot, PAD : PAD + coarse_rows, :] = odd
            tail = jnp.where(line == coarse_rows - 1, odd, 0.0)
            value = even + odd + ones[slot, PAD - 1 : PAD - 1 + coarse_rows, :] + tail
            if k >= 3:
                value = value * 0.25
            at = (k * half + z) * share
            for b in range(shots):
                blocks[b, at : at + share, :] = value[b * share : (b + 1) * share, :]
    for j in range(shots):
        chunks[j][...] = blocks[shot_index ^ j, 0 : channels * half * share, :]


def finish(*refs, steps):
    parts, out_ref = refs[:-1], refs[-1]
    channels, depth_len, rows, columns = out_ref.shape
    total = parts[0][...]
    for part in parts[1:]:
        total = total + part[...]
    coarse = exact_dot(total, refine_matrix(columns), ((1,), (1,))) / steps
    for k in range(channels):
        for z in range(depth_len):
            at = (k * depth_len + z) * rows
            out_ref[k, z] = coarse[at : at + rows, :]


def local_part(
    forward, adjoint_last, adjoint_late, residuals, source_cells, receiver_cells, assignment, model
):
    steps = forward.shape[0]
    shots_here, depth_len, rows, columns = adjoint_last.shape
    channels, coarse_len, share, coarse_columns = model.shape
    shots = lax.axis_size("shot")
    depth_count = lax.axis_size("depth")
    reach = (steps + 1) // 2
    assert shots_here == 1 and depth_count % 2 == 0 and shots & (shots - 1) == 0
    assert depth_len > steps and coarse_len >= reach and share * shots * 2 == rows
    f32 = jnp.float32
    shape = lambda *dims: jax.ShapeDtypeStruct(dims, f32)
    local = lambda *dims: pltpu.VMEM(dims, f32)
    near = lambda array: pltpu.with_memory_space_constraint(array, pltpu.VMEM)
    far = lambda array: pltpu.with_memory_space_constraint(array, pltpu.HBM)
    first_pairs = [(i, i ^ 1) for i in range(depth_count)]
    second_pairs = [(i, (i + 1 if i % 2 else i - 1) % depth_count) for i in range(depth_count)]

    def moved(array, axis, pairs):
        return near(lax.ppermute(array, axis, pairs))

    part = reach * channels * share
    own_rows = coarse_len * channels * share
    halo = 3 * steps + 1
    own, model_first, model_second, field_first, field_second = pl.pallas_call(
        functools.partial(pack, steps=steps, reach=reach),
        in_specs=[HBM] * 4,
        out_specs=[VMEM] * 5,
        out_shape=[
            local(own_rows, columns),
            local(part, columns),
            local(part, columns),
            local(halo, rows, columns),
            local(halo, rows, columns),
        ],
        scratch_shapes=[
            pltpu.VMEM((channels, coarse_len, share, coarse_columns), f32),
            pltpu.VMEM((own_rows, coarse_columns), f32),
            pltpu.VMEM((steps, rows, columns), jnp.bfloat16),
            pltpu.SemaphoreType.DMA((6,)),
        ],
        name="pack",
        compiler_params=LIMIT,
    )(far(model), far(adjoint_last), far(adjoint_late), far(forward))
    model_second = moved(model_second, "depth", second_pairs)
    model_first = moved(model_first, "depth", first_pairs)
    field_second = moved(field_second, "depth", second_pairs)
    field_first = moved(field_first, "depth", first_pairs)
    height = depth_len + 2 * steps + 1
    added = pl.pallas_call(
        functools.partial(injection, steps=steps, depth_len=depth_len, rows=rows),
        in_specs=[SMEM, VMEM, VMEM],
        out_specs=VMEM,
        out_shape=local(steps, height - 2, rows, columns),
        name="injection",
        compiler_params=LIMIT,
    )(far(assignment), far(residuals), far(receiver_cells.transpose(2, 0, 1)))
    joined_rows = own_rows + 2 * part
    joined = pl.pallas_call(
        functools.partial(join_model, layer=channels * share, depth_count=depth_count),
        in_specs=[VMEM] * 3,
        out_specs=VMEM,
        out_shape=local(joined_rows, columns),
        name="join_model",
        compiler_params=LIMIT,
    )(near(own), model_first, model_second)
    swap = lambda array, j: moved(array, "shot", [(i, i ^ j) for i in range(shots)])
    gathered = [near(joined)] + [swap(joined, j) for j in range(1, shots)]
    padded = rows + 2 * PAD
    prepared = pl.pallas_call(
        functools.partial(prepare, steps=steps, depth_count=depth_count),
        in_specs=[VMEM] * 6,
        out_specs=[VMEM] * 5,
        out_shape=[
            local(height, padded, columns),
            local(channels, height - 2, rows, columns),
            local(height - 2, rows, columns),
            local(channels, depth_len + 1, rows, columns),
            local(steps, depth_len + 1, rows, columns),
        ],
        scratch_shapes=[
            pltpu.VMEM((height, padded, columns), f32),
            pltpu.VMEM((height, rows, columns), f32),
            pltpu.VMEM((height, rows, columns), f32),
        ],
        name="prepare",
        compiler_params=LIMIT,
    )(adjoint_last, adjoint_late, forward, field_first, field_second, near(added))
    layers = coarse_len + 2 * reach
    chunk = local(channels * coarse_len * share, columns)
    final, *chunks = pl.pallas_call(
        functools.partial(march, steps=steps, shots=shots, depth_count=depth_count, reach=reach),
        in_specs=[SMEM, SMEM] + [VMEM] * (6 + shots),
        out_specs=[VMEM] * (1 + shots),
        out_shape=[shape(1, depth_len, rows, columns)] + [chunk] * shots,
        scratch_shapes=[
            pltpu.VMEM((shots, joined_rows, columns), f32),
            pltpu.VMEM((layers, channels, rows // 2 + PAD, columns), f32),
            pltpu.VMEM((layers, channels, rows, columns), f32),
            pltpu.VMEM((layers - 1, channels, rows, columns), f32),
            pltpu.VMEM((height, padded, columns), f32),
            pltpu.VMEM((height, padded, columns), f32),
            pltpu.VMEM((height, padded, columns), f32),
            pltpu.VMEM((height, rows, columns), f32),
            pltpu.VMEM((channels, depth_len + 1, rows, columns), f32),
            pltpu.VMEM((4, rows, columns), f32),
        ],
        name="march",
        compiler_params=LIMIT,
    )(
        far(assignment),
        far(source_cells),
        *map(near, prepared),
        near(added),
        *gathered,
    )
    parts = [near(chunks[0])] + [swap(chunks[j], j) for j in range(1, shots)]
    gradients = pl.pallas_call(
        functools.partial(finish, steps=steps),
        in_specs=[VMEM] * shots,
        out_specs=VMEM,
        out_shape=shape(*model.shape),
        name="finish",
        compiler_params=LIMIT,
    )(*parts)
    return final, gradients


def solution(mesh):
    placed = (
        P(None, ("grp", "shot"), "depth", None, None),
        P(("grp", "shot"), "depth", None, None),
        P(("grp", "shot"), "depth", None, None),
        P(("grp", "shot"), None, None),
        P("grp", None),
        P("grp", None, None),
        P("grp"),
        P(None, ("grp", "depth"), "shot", None),
    )
    return jax.shard_map(
        local_part,
        mesh=mesh,
        in_specs=placed,
        out_specs=(
            P(("grp", "shot"), "depth", None, None),
            P(None, ("grp", "depth"), "shot", None),
        ),
        check_vma=False,
    )
```

time: 43.9 us -> 36.3 us (0.83)
  Pallas kernels: 13.5 us -> 7.04 us
  local copies, waits for them, and re-layouts: 2.65 us -> 0.01 us
  waiting for transfers between devices: 14.8 us -> 16.2 us
    pallas_call x6, Pallas kernels: 13.5 us -> 7.04 us  [the longest x1 2.97 us: local_part(): pl.pallas_call(functools.partial(march, steps=steps, shots=shots, depth_c...]
    unnamed x20 -> x6, local copies, waits for them, and re-layouts: 2.65 us -> 0.01 us
    ppermute x10, waiting for transfers between devices: 14.8 us -> 16.2 us  [moved(): return near(lax.ppermute(array, axis, pairs))]
  transfers between devices with their start and end apart: 10 -> 10, of which waited for: 7 -> 5; matrix products, arithmetic and copies ran while one was open for 0% -> 0% of each run, Pallas kernels for 13% -> 6%
where the time goes in v2:
time: 36.3 us; the launch traced here: 36.1 us
  waiting for transfers between devices  16.2 us (45%)
  starting transfers between devices  12.1 us (33%)
  Pallas kernels  7.04 us (19%)
  between operations  0.74 us (2%)
    ppermute x10, waiting for transfers between devices, moved(): return near(lax.ppermute(array, axis, pairs))  16.2 us
    ppermute x10, starting transfers between devices, moved(): return near(lax.ppermute(array, axis, pairs))  12.1 us
    pallas_call x1, Pallas kernels, local_part(): pl.pallas_call(functools.partial(march, steps=steps, shots=shots, depth_c...  2.97 us
    pallas_call x1, Pallas kernels, local_part(): pl.pallas_call(functools.partial(injection, steps=steps, depth_len=depth_...  1.66 us
    pallas_call x1, Pallas kernels, local_part(): pl.pallas_call(functools.partial(pack, steps=steps, reach=reach), in_spec...  1.12 us
    pallas_call x1, Pallas kernels, local_part(): pl.pallas_call(functools.partial(finish, steps=steps), in_specs=[VMEM] *...  0.82 us
  transfers between devices with their start and end apart: 10, of which 5 were waited for; matrix products, arithmetic and copies ran while one was open for 0% of the time, Pallas kernels for 6%

profile of v2, /device:TPU:0, one launch (start us, length us, event | category | flops | bytes accessed | tf_op | source)
XLA Modules:
  0.0 36.1 jit_solution(5028920448770215415)
XLA Ops:
  0.6 0.0 copy-start.1
  0.6 0.0 copy-start.2
  0.7 0.0 copy-start
  0.7 1.1 %pack.1 = (f32[96,128]{1,0:T(8,128)S(1)}, f32[48,128]{1,0:T(8,128)S(1)}, f32[48,128]{1,0:T(8,128)S(1)}, f32[13,32,128]{2,1,0:T(8,128)S(1)}, f32[13,32,128]{2,1,0:T(8,128)S(1)}) custom-call(f32[6,4,4,64]{3,2,1,0:T(4,128)} %model_ref.1, f32[1,8,32,128]{3,2,1,0:T(8,128)} %current_ref.3, f32[1,8,32,128]{3,2,1,0:T(8,128)} %previous_ref.3, ...), custom_call_target="tpu_custom_call" | custom-call | tf_op jit(solution)/shard_map/pack/pallas_call | solution.py:460
  1.8 0.6 %collective-permute-start = (f32[13,32,128]{2,1,0:T(8,128)S(1)}, f32[13,32,128]{2,1,0:T(8,128)S(1)}, u32[]{:S(2)}, u32[]{:S(2)}) collective-permute-start(f32[13,32,128]{2,1,0:T(8,128)S(1)} %get-tuple-element.17), channel_id=1, source_target_pairs={{0,4},{4,0},{8,12},{12,8},{1,5},{5,1},{9,13},{13,9},{2,6},{6,2},{1... | collective-permute-start | bytes 638984 | tf_op jit(solution)/shard_map/ppermute | solution.py:455
  2.3 2.6 %collective-permute-start.1 = (f32[13,32,128]{2,1,0:T(8,128)S(1)}, f32[13,32,128]{2,1,0:T(8,128)S(1)}, u32[]{:S(2)}, u32[]{:S(2)}) collective-permute-start(f32[13,32,128]{2,1,0:T(8,128)S(1)} %get-tuple-element.18), channel_id=1, source_target_pairs={{0,12},{4,8},{8,4},{12,0},{1,13},{5,9},{9,5},{13,1},{2,14},{6,10},... | collective-permute-start | bytes 638984 | tf_op jit(solution)/shard_map/ppermute | solution.py:455
  4.9 0.1 collective-permute-start.2
  5.0 0.1 collective-permute-start.3
  5.1 1.0 %collective-permute-done.2.first_ref = f32[48,128]{1,0:T(8,128)S(1)} collective-permute-done((f32[48,128]{1,0:T(8,128)S(1)}, f32[48,128]{1,0:T(8,128)S(1)}, u32[]{:S(2)}, u32[]{:S(2)}) %collective-permute-start.2) | collective-permute-done | bytes 24608 | tf_op jit(solution)/shard_map/ppermute | solution.py:455
  6.1 4.9 %collective-permute-done.3.second_ref = f32[48,128]{1,0:T(8,128)S(1)} collective-permute-done((f32[48,128]{1,0:T(8,128)S(1)}, f32[48,128]{1,0:T(8,128)S(1)}, u32[]{:S(2)}, u32[]{:S(2)}) %collective-permute-start.3) | collective-permute-done | bytes 24608 | tf_op jit(solution)/shard_map/ppermute | solution.py:455
  11.0 1.5 %collective-permute-start.4 = (f32[192,128]{1,0:T(8,128)S(1)}, f32[192,128]{1,0:T(8,128)S(1)}, u32[]{:S(2)}, u32[]{:S(2)}) collective-permute-start(f32[192,128]{1,0:T(8,128)S(1)} %join_model.1.refs_0_), channel_id=1, source_target_pairs={{0,1},{1,0},{2,3},{3,2},{4,5},{5,4},{6,7},{7,6},{8,9},{9,8},{10,11... | collective-permute-start | bytes 294920 | tf_op jit(solution)/shard_map/ppermute | solution.py:455
  12.5 2.6 %collective-permute-start.5 = (f32[192,128]{1,0:T(8,128)S(1)}, f32[192,128]{1,0:T(8,128)S(1)}, u32[]{:S(2)}, u32[]{:S(2)}) collective-permute-start(f32[192,128]{1,0:T(8,128)S(1)} %join_model.1.refs_0_), channel_id=1, source_target_pairs={{0,2},{1,3},{2,0},{3,1},{4,6},{5,7},{6,4},{7,5},{8,10},{9,11},{10,... | collective-permute-start | bytes 294920 | tf_op jit(solution)/shard_map/ppermute | solution.py:455
  15.1 0.4 collective-permute-start.6
  15.5 1.7 %injection.1.added_ref = f32[4,15,32,128]{3,2,1,0:T(8,128)S(1)} custom-call(s32[4]{0:T(128)} %assign_ref.3, f32[1,4,256]{2,1,0:T(4,128)} %residual_ref.1, s32[3,4,256]{2,1,0:T(4,128)} %bitcast.1), custom_call_target="tpu_custom_call" | custom-call | tf_op jit(solution)/shard_map/injection/pallas_call | solution.py:485
  17.2 0.0 collective-permute-done.first_ref
  17.2 0.0 collective-permute-done.1.second_ref
  17.2 0.0 copy-done.1
  17.2 0.0 copy-done.2
  17.2 0.0 copy-done
  17.2 0.5 %prepare.1 = (f32[17,48,128]{2,1,0:T(8,128)S(1)}, f32[6,15,32,128]{3,2,1,0:T(8,128)S(1)}, f32[15,32,128]{2,1,0:T(8,128)S(1)}, f32[6,9,32,128]{3,2,1,0:T(8,128)S(1)}, f32[4,9,32,128]{3,2,1,0:T(8,128)S(1)}) custom-call(f32[1,8,32,128]{3,2,1,0:T(8,128)S(1)} %copy-done.1, f32[1,8,32,128]{3,2,1,0:T(8,128)S(1)} %copy-done.2, ...), custom_call_target="tpu_custom_call" | custom-call | tf_op jit(solution)/shard_map/prepare/pallas_call | solution.py:505
  17.7 0.0 collective-permute-done.4.refs_1_
  17.7 5.6 %collective-permute-done.5.refs_2_ = f32[192,128]{1,0:T(8,128)S(1)} collective-permute-done((f32[192,128]{1,0:T(8,128)S(1)}, f32[192,128]{1,0:T(8,128)S(1)}, u32[]{:S(2)}, u32[]{:S(2)}) %collective-permute-start.5) | collective-permute-done | bytes 98336 | tf_op jit(solution)/shard_map/ppermute | solution.py:455
  23.3 0.0 collective-permute-done.6.refs_3_
  23.3 3.0 %march.1 = (f32[1,8,32,128]{3,2,1,0:T(8,128)}, f32[96,128]{1,0:T(8,128)S(1)}, f32[96,128]{1,0:T(8,128)S(1)}, f32[96,128]{1,0:T(8,128)S(1)}, f32[96,128]{1,0:T(8,128)S(1)}) custom-call(s32[4]{0:T(128)} %assign_ref.3, s32[4,3]{1,0:T(4,128)} %source_ref.1, f32[17,48,128]{2,1,0:T(8,128)S(1)} %get-tuple-element.19.field, ...), custom_call_target="tpu_custom_call" | custom-call | tf_op jit(solution)/shard_map/march/pallas_call | solution.py:526
  26.3 1.9 %collective-permute-start.7 = (f32[96,128]{1,0:T(8,128)S(1)}, f32[96,128]{1,0:T(8,128)S(1)}, u32[]{:S(2)}, u32[]{:S(2)}) collective-permute-start(f32[96,128]{1,0:T(8,128)S(1)} %get-tuple-element.29), channel_id=1, source_target_pairs={{0,1},{1,0},{2,3},{3,2},{4,5},{5,4},{6,7},{7,6},{8,9},{9,8},{10,11... | collective-permute-start | bytes 147464 | tf_op jit(solution)/shard_map/ppermute | solution.py:455
  28.1 1.2 %collective-permute-start.8 = (f32[96,128]{1,0:T(8,128)S(1)}, f32[96,128]{1,0:T(8,128)S(1)}, u32[]{:S(2)}, u32[]{:S(2)}) collective-permute-start(f32[96,128]{1,0:T(8,128)S(1)} %get-tuple-element.30), channel_id=1, source_target_pairs={{0,2},{1,3},{2,0},{3,1},{4,6},{5,7},{6,4},{7,5},{8,10},{9,11},{10,... | collective-permute-start | bytes 147464 | tf_op jit(solution)/shard_map/ppermute | solution.py:455
  29.4 1.3 %collective-permute-start.9 = (f32[96,128]{1,0:T(8,128)S(1)}, f32[96,128]{1,0:T(8,128)S(1)}, u32[]{:S(2)}, u32[]{:S(2)}) collective-permute-start(f32[96,128]{1,0:T(8,128)S(1)} %get-tuple-element.31), channel_id=1, source_target_pairs={{0,3},{1,2},{2,1},{3,0},{4,7},{5,6},{6,5},{7,4},{8,11},{9,10},{10,... | collective-permute-start | bytes 147464 | tf_op jit(solution)/shard_map/ppermute | solution.py:455
  30.7 0.0 collective-permute-done.7.refs_1_
  30.7 3.5 %collective-permute-done.8.refs_2_ = f32[96,128]{1,0:T(8,128)S(1)} collective-permute-done((f32[96,128]{1,0:T(8,128)S(1)}, f32[96,128]{1,0:T(8,128)S(1)}, u32[]{:S(2)}, u32[]{:S(2)}) %collective-permute-start.8) | collective-permute-done | bytes 49184 | tf_op jit(solution)/shard_map/ppermute | solution.py:455
  34.2 1.1 %collective-permute-done.9.refs_3_ = f32[96,128]{1,0:T(8,128)S(1)} collective-permute-done((f32[96,128]{1,0:T(8,128)S(1)}, f32[96,128]{1,0:T(8,128)S(1)}, u32[]{:S(2)}, u32[]{:S(2)}) %collective-permute-start.9) | collective-permute-done | bytes 49184 | tf_op jit(solution)/shard_map/ppermute | solution.py:455
  35.3 0.8 %finish.1 = f32[6,4,4,64]{3,2,1,0:T(4,128)} custom-call(f32[96,128]{1,0:T(8,128)S(1)} %get-tuple-element.28.refs_0_, f32[96,128]{1,0:T(8,128)S(1)} %collective-permute-done.7.refs_1_, f32[96,128]{1,0:T(8,128)S(1)} %collective-permute-done.8.refs_2_, f32[96,128]{1,0:T(8,128)S(1)} %collective-permute-done.9.refs_3_), custom_call_target="tpu_custom_call" | custom-call | tf_op jit(solution)/shard_map/finish/pallas_call | solution.py:553
  (1 shorter events, 0.0 us)
Async XLA Ops:
  0.6 16.5 %copy-start.1 = (f32[1,8,32,128]{3,2,1,0:T(8,128)S(1)}, f32[1,8,32,128]{3,2,1,0:T(8,128)}, u32[]{:S(2)}) copy-start(f32[1,8,32,128]{3,2,1,0:T(8,128)} %current_ref.3) | copy-start | bytes 393220
  0.6 16.5 %copy-start.2 = (f32[1,8,32,128]{3,2,1,0:T(8,128)S(1)}, f32[1,8,32,128]{3,2,1,0:T(8,128)}, u32[]{:S(2)}) copy-start(f32[1,8,32,128]{3,2,1,0:T(8,128)} %previous_ref.3) | copy-start | bytes 393220
  0.7 16.5 %copy-start = (bf16[4,1,8,32,128]{4,3,2,1,0:T(8,128)(2,1)S(1)}, bf16[4,1,8,32,128]{4,3,2,1,0:T(8,128)(2,1)}, u32[]{:S(2)}) copy-start(bf16[4,1,8,32,128]{4,3,2,1,0:T(8,128)(2,1)} %forward_ref.3) | copy-start | bytes 786436
  1.8 15.4 %collective-permute-start = (f32[13,32,128]{2,1,0:T(8,128)S(1)}, f32[13,32,128]{2,1,0:T(8,128)S(1)}, u32[]{:S(2)}, u32[]{:S(2)}) collective-permute-start(f32[13,32,128]{2,1,0:T(8,128)S(1)} %get-tuple-element.17), channel_id=1, source_target_pairs={{0,4},{4,0},{8,12},{12,8},{1,5},{5,1},{9,13},{13,9},{2,6},{6,2},{1... | collective-permute-start | bytes 638984 | tf_op jit(solution)/shard_map/ppermute | solution.py:455
  2.3 14.8 %collective-permute-start.1 = (f32[13,32,128]{2,1,0:T(8,128)S(1)}, f32[13,32,128]{2,1,0:T(8,128)S(1)}, u32[]{:S(2)}, u32[]{:S(2)}) collective-permute-start(f32[13,32,128]{2,1,0:T(8,128)S(1)} %get-tuple-element.18), channel_id=1, source_target_pairs={{0,12},{4,8},{8,4},{12,0},{1,13},{5,9},{9,5},{13,1},{2,14},{6,10},... | collective-permute-start | bytes 638984 | tf_op jit(solution)/shard_map/ppermute | solution.py:455
  4.9 1.2 %collective-permute-start.2 = (f32[48,128]{1,0:T(8,128)S(1)}, f32[48,128]{1,0:T(8,128)S(1)}, u32[]{:S(2)}, u32[]{:S(2)}) collective-permute-start(f32[48,128]{1,0:T(8,128)S(1)} %get-tuple-element.25), channel_id=1, source_target_pairs={{0,4},{4,0},{8,12},{12,8},{1,5},{5,1},{9,13},{13,9},{2,6},{6,2},{1... | collective-permute-start | bytes 73736 | tf_op jit(solution)/shard_map/ppermute | solution.py:455
  5.0 6.0 %collective-permute-start.3 = (f32[48,128]{1,0:T(8,128)S(1)}, f32[48,128]{1,0:T(8,128)S(1)}, u32[]{:S(2)}, u32[]{:S(2)}) collective-permute-start(f32[48,128]{1,0:T(8,128)S(1)} %get-tuple-element.26), channel_id=1, source_target_pairs={{0,12},{4,8},{8,4},{12,0},{1,13},{5,9},{9,5},{13,1},{2,14},{6,10},... | collective-permute-start | bytes 73736 | tf_op jit(solution)/shard_map/ppermute | solution.py:455
  11.0 6.6 %collective-permute-start.4 = (f32[192,128]{1,0:T(8,128)S(1)}, f32[192,128]{1,0:T(8,128)S(1)}, u32[]{:S(2)}, u32[]{:S(2)}) collective-permute-start(f32[192,128]{1,0:T(8,128)S(1)} %join_model.1.refs_0_), channel_id=1, source_target_pairs={{0,1},{1,0},{2,3},{3,2},{4,5},{5,4},{6,7},{7,6},{8,9},{9,8},{10,11... | collective-permute-start | bytes 294920 | tf_op jit(solution)/shard_map/ppermute | solution.py:455
  12.5 10.8 %collective-permute-start.5 = (f32[192,128]{1,0:T(8,128)S(1)}, f32[192,128]{1,0:T(8,128)S(1)}, u32[]{:S(2)}, u32[]{:S(2)}) collective-permute-start(f32[192,128]{1,0:T(8,128)S(1)} %join_model.1.refs_0_), channel_id=1, source_target_pairs={{0,2},{1,3},{2,0},{3,1},{4,6},{5,7},{6,4},{7,5},{8,10},{9,11},{10,... | collective-permute-start | bytes 294920 | tf_op jit(solution)/shard_map/ppermute | solution.py:455
  15.1 8.2 %collective-permute-start.6 = (f32[192,128]{1,0:T(8,128)S(1)}, f32[192,128]{1,0:T(8,128)S(1)}, u32[]{:S(2)}, u32[]{:S(2)}) collective-permute-start(f32[192,128]{1,0:T(8,128)S(1)} %join_model.1.refs_0_), channel_id=1, source_target_pairs={{0,3},{1,2},{2,1},{3,0},{4,7},{5,6},{6,5},{7,4},{8,11},{9,10},{10,... | collective-permute-start | bytes 294920 | tf_op jit(solution)/shard_map/ppermute | solution.py:455
  26.3 4.4 %collective-permute-start.7 = (f32[96,128]{1,0:T(8,128)S(1)}, f32[96,128]{1,0:T(8,128)S(1)}, u32[]{:S(2)}, u32[]{:S(2)}) collective-permute-start(f32[96,128]{1,0:T(8,128)S(1)} %get-tuple-element.29), channel_id=1, source_target_pairs={{0,1},{1,0},{2,3},{3,2},{4,5},{5,4},{6,7},{7,6},{8,9},{9,8},{10,11... | collective-permute-start | bytes 147464 | tf_op jit(solution)/shard_map/ppermute | solution.py:455
  28.1 6.0 %collective-permute-start.8 = (f32[96,128]{1,0:T(8,128)S(1)}, f32[96,128]{1,0:T(8,128)S(1)}, u32[]{:S(2)}, u32[]{:S(2)}) collective-permute-start(f32[96,128]{1,0:T(8,128)S(1)} %get-tuple-element.30), channel_id=1, source_target_pairs={{0,2},{1,3},{2,0},{3,1},{4,6},{5,7},{6,4},{7,5},{8,10},{9,11},{10,... | collective-permute-start | bytes 147464 | tf_op jit(solution)/shard_map/ppermute | solution.py:455
  29.4 5.9 %collective-permute-start.9 = (f32[96,128]{1,0:T(8,128)S(1)}, f32[96,128]{1,0:T(8,128)S(1)}, u32[]{:S(2)}, u32[]{:S(2)}) collective-permute-start(f32[96,128]{1,0:T(8,128)S(1)} %get-tuple-element.31), channel_id=1, source_target_pairs={{0,3},{1,2},{2,1},{3,0},{4,7},{5,6},{6,5},{7,4},{8,11},{9,10},{10,... | collective-permute-start | bytes 147464 | tf_op jit(solution)/shard_map/ppermute | solution.py:455
